TPU v7x, 32 devices: a whole 2x2x4 slice. The times are simulated.
32 devices in a mesh: py: 4 (over y, x), pz: 8 (over z, core).
Axes of the slice: x: 2, y: 2, z: 4, core: 2. Of those that a mesh axis runs over, the one named last changes fastest.
Arguments:
- positions: float32 [3, 131072], P(None, ('py', 'pz')), may hold values from 0 to 512, as said below
- masses: float32 [131072], P(('py', 'pz')), may hold values from 16 to 160
Outputs:
- forces: float32 [3, 32, 64, 512], P(None, 'py', 'pz')
Inputs may be any that keep to these rules, and one draw needn't show every extreme that they name: `positions`: the particles come in blocks of 4096 columns; in the block numbered a 8 + b, row 0 lies in [a 8, (a + 1) * 8), row 1 in [b * 8, (b + 1) * 8), and row 2 in [0, 512).
All inputs are finite; a program needn't handle non-finite values.
Results may differ from a plain program's by a relative error of at most 0.0003.
Values sent between devices are 32-bit elements; how exact they have to be, the bound alone decides.
A program may use at most 64 MiB of HBM per device.

v0:
```python
import functools
import math

import jax
import jax.numpy as jnp
import ml_dtypes
import numpy as np
from jax import lax
from jax.experimental import pallas as pl
from jax.experimental.pallas import tpu as pltpu
from jax.sharding import PartitionSpec as P

MESH = pl.DeviceIdType.MESH
F32 = jnp.float32
BF16 = jnp.bfloat16
SMOOTHING_SQ = 0.25
CELL = 8
PAIR = 2 * CELL
GROUPS = 128 // PAIR


def parts(table, count):
    out = []
    for _ in range(count):
        out.append(table.astype(ml_dtypes.bfloat16))
        table = table - out[-1].astype(np.float64)
    return np.stack(out)


def tables(n_py, n_pz, nx, nf):
    ny, nz = CELL * n_py, CELL * n_pz
    kept = nx // 2
    phase = (np.outer(np.arange(kept), np.arange(nx)) % nx) * (2 * np.pi / nx)
    line = np.concatenate([np.cos(phase), -np.sin(phase)])
    phase = (np.outer(np.arange(ny), np.arange(ny)) % ny) * (2 * np.pi / ny)
    eye = np.eye(nf)
    rows = np.concatenate([np.kron(np.cos(phase), eye), np.kron(np.sin(phase), eye)], axis=1)
    phase = (np.outer(np.arange(nz), np.arange(nz)) % nz) * (2 * np.pi / nz)
    cos, sin = np.cos(phase), np.sin(phase)
    forward = np.zeros((n_pz, 2, CELL, 2, nz))
    forward[:, 0, :, 0] = cos.reshape(n_pz, CELL, nz)
    forward[:, 0, :, 1] = -sin.reshape(n_pz, CELL, nz)
    forward[:, 1, :, 0] = sin.reshape(n_pz, CELL, nz)
    forward[:, 1, :, 1] = cos.reshape(n_pz, CELL, nz)
    forward = forward.reshape(2 * nz, 2, nz)
    turned = np.stack([forward[:, 1], -forward[:, 0]], axis=1)
    forward = np.concatenate([forward.reshape(2 * nz, 2 * nz), turned.reshape(2 * nz, 2 * nz)], 1)
    inverse = np.zeros((2, nz, n_pz, 2, CELL))
    inverse[0, :, :, 0] = cos.reshape(nz, n_pz, CELL)
    inverse[0, :, :, 1] = sin.reshape(nz, n_pz, CELL)
    inverse[1, :, :, 0] = -sin.reshape(nz, n_pz, CELL)
    inverse[1, :, :, 1] = cos.reshape(nz, n_pz, CELL)
    inverse = inverse.reshape(2 * nz, n_pz, 2, CELL)
    turned = np.stack([-inverse[:, :, 1], inverse[:, :, 0]], axis=2)
    inverse = np.concatenate([inverse.reshape(2 * nz, 2 * nz), turned.reshape(2 * nz, 2 * nz)], 1)
    return parts(line, 3), parts(rows, 3), parts(forward, 2), parts(inverse, 3)


def split(x, count=2):
    out = []
    for i in range(count):
        out.append(x.astype(BF16))
        if i < count - 1:
            x = x - out[-1].astype(F32)
    return out


def dot_parts(left, right, dims=((1,), (0,))):
    count = len(left)
    total = None
    for order in reversed(range(count)):
        for i in range(order + 1):
            term = lax.dot_general(
                left[i], right[order - i], (dims, ((), ())), preferred_element_type=F32
            )
            total = term if total is None else total + term
    return total


def swap_groups(tiles):
    group = lax.broadcasted_iota(jnp.int32, tiles[0].shape, 1) // PAIR
    moved = []
    for step in range(GROUPS):
        mixed = tiles[step]
        for a in range(1, GROUPS):
            mixed = jnp.where(group == a, tiles[(a + step) % GROUPS], mixed)
        moved.append(pltpu.roll(mixed, step * PAIR, 1) if step else mixed)
    out = []
    for a in range(GROUPS):
        mixed = moved[(0 - a) % GROUPS]
        for g in range(1, GROUPS):
            mixed = jnp.where(group == g, moved[(g - a) % GROUPS], mixed)
        out.append(mixed)
    return out


def green_factor(rank, n_py, n_pz, nx, nf):
    ny, nz = CELL * n_py, CELL * n_pz
    shape = (ny * nf, 2 * nz)
    row = lax.broadcasted_iota(jnp.int32, shape, 0)
    col = lax.broadcasted_iota(jnp.int32, shape, 1)

    def square(wave, period):
        folded = jnp.minimum(wave, period - wave).astype(F32)
        return (folded * (2.0 * math.pi / period)) ** 2

    wave_x = rank * nf + row % nf
    total = square(row // nf, ny) + square(col % nz, nz) + square(wave_x, nx)
    safe = jnp.where(total > 0, total, 1.0)
    green = jnp.where(total > 0, -4.0 * math.pi * jnp.exp(-SMOOTHING_SQ * total) / safe, 0.0)
    return green * (jnp.where(wave_x > 0, 2.0, 1.0) * (1.0 / float(ny * nz * nx)))


def kernel(
    n_py, n_pz, nx, nf, chunk,
    pos_hbm, mass_hbm, line_hbm, rows_hbm, fwd_hbm, inv_hbm,
    out_ref,
    pos_ref, mass_ref, line, rows, fwd, inv, table_sem,
    hot, acc_halo, acc, halo_out, halo_in, halo_send, halo_recv,
    send1, recv1, field, send2, recv2, waves,
    send_sem1, recv_sem1, send_sem2, recv_sem2,
    edge_out, edge_in, edge_send, edge_recv,
):
    n = n_py * n_pz
    my_y, my_z = lax.axis_index("py"), lax.axis_index("pz")
    rank = my_y * n_pz + my_z

    loads = [
        pltpu.make_async_copy(src, dst, table_sem.at[i])
        for i, (src, dst) in enumerate(
            [
                (pos_hbm, pos_ref),
                (mass_hbm, mass_ref),
                (line_hbm, line),
                (rows_hbm, rows),
                (fwd_hbm, fwd),
                (inv_hbm, inv),
            ]
        )
    ]
    for load in loads:
        load.start()

    def coords(step):
        other_y = lax.rem(n - step, n_py) ^ my_y
        other_z = ((n - step) // n_py) ^ my_z
        return other_y * n_pz + other_z, (other_y, other_z)

    barrier = pltpu.get_barrier_semaphore()

    @pl.loop(1, n)
    def _(step):
        pl.semaphore_signal(barrier, inc=1, device_id=coords(step)[1], device_id_type=MESH)

    base_y = (my_y * CELL).astype(F32)
    base_z = (my_z * CELL).astype(F32)
    acc[...] = jnp.zeros_like(acc)
    acc_halo[...] = jnp.zeros_like(acc_halo)
    cell = lax.broadcasted_iota(jnp.int32, (CELL, chunk), 0).astype(F32)
    x_index = lax.broadcasted_iota(jnp.int32, (nx, chunk), 0).astype(F32)

    for load in loads[:2]:
        load.wait()

    def weights(turn):
        span = pl.ds(pl.multiple_of(turn * chunk, chunk), chunk)
        along_y = pos_ref[0:1, span] - base_y
        along_z = pos_ref[1:2, span] - base_z
        along_x = pos_ref[2:3, span]
        mass = mass_ref[0:1, span]
        floor_x = jnp.floor(along_x)
        frac_x = along_x - floor_x
        hat_y = jnp.maximum(1.0 - jnp.abs(along_y - cell), 0.0)
        hat_z = jnp.maximum(1.0 - jnp.abs(along_z - cell), 0.0)
        last_y = jnp.maximum(along_y - (CELL - 1.0), 0.0)
        last_z = jnp.maximum(along_z - (CELL - 1.0), 0.0)
        shares = (mass * (1.0 - frac_x), mass * frac_x)
        return span, floor_x, hat_y, hat_z, last_y, last_z, shares

    def deposited(tile_sets, one_hot):
        pairs = [split(jnp.concatenate(tiles, axis=0)) for tiles in tile_sets]
        stacked = jnp.concatenate([pair[i] for i in range(2) for pair in pairs], axis=0)
        return lax.dot_general(
            stacked, one_hot, (((1,), (1,)), ((), ())), preferred_element_type=F32
        )

    def settled(sums):
        plane = sums.shape[0] // 4
        lower = sums[0:plane] + sums[2 * plane : 3 * plane]
        upper = sums[plane : 2 * plane] + sums[3 * plane : 4 * plane]
        return lower + pltpu.roll(upper, 1, 1)

    turns = pos_ref.shape[1] // chunk

    @pl.loop(0, turns)
    def _(turn):
        span, floor_x, hat_y, hat_z, last_y, last_z, shares = weights(turn)
        one_hot = jnp.where(x_index == floor_x, 1.0, 0.0).astype(BF16)
        hot[:, span] = one_hot
        tile_sets = [
            [
                last_y * (hat_z * share),
                hat_y * (last_z * share),
                jnp.where(cell == 0.0, last_y * (last_z * share), 0.0),
            ]
            for share in shares
        ]
        acc_halo[...] += deposited(tile_sets, one_hot)

    outer = settled(acc_halo[...])
    for i in range(3):
        halo_out[i] = outer[i * CELL : (i + 1) * CELL]

    up_y, up_z = lax.rem(my_y + 1, n_py), lax.rem(my_z + 1, n_pz)
    down_y, down_z = lax.rem(my_y + n_py - 1, n_py), lax.rem(my_z + n_pz - 1, n_pz)
    pl.semaphore_wait(barrier, n - 1)
    halos = [
        pltpu.make_async_remote_copy(
            src_ref=halo_out.at[i],
            dst_ref=halo_in.at[i],
            send_sem=halo_send.at[i],
            recv_sem=halo_recv.at[i],
            device_id=target,
            device_id_type=MESH,
        )
        for i, target in enumerate([(up_y, my_z), (my_y, up_z), (up_y, up_z)])
    ]
    for halo in halos:
        halo.start()

    @pl.loop(0, turns)
    def _(turn):
        span, _, hat_y, hat_z, _, _, shares = weights(turn)
        tile_sets = []
        for share in shares:
            scaled = hat_z * share
            tile_sets.append([hat_y[a : a + 1] * scaled for a in range(CELL)])
        acc[...] += deposited(tile_sets, hot[:, span])

    grid = settled(acc[...])
    green = green_factor(rank, n_py, n_pz, nx, nf)
    for load in loads[2:]:
        load.wait()
    for halo in halos:
        halo.wait()

    first = lax.broadcasted_iota(jnp.int32, (CELL, nx), 0) == 0
    beside = halo_in[1]
    doubled = []
    for a in range(CELL):
        tile = grid[a * CELL : (a + 1) * CELL]
        tile = tile + jnp.where(first, beside[a : a + 1], 0.0)
        if a == 0:
            tile = tile + halo_in[0] + jnp.where(first, halo_in[2], 0.0)
        doubled += [tile, tile]
    density = split(jnp.concatenate(doubled, axis=0))
    kept = nx // 2
    both = dot_parts([line[0], line[1]], density, ((1,), (1,)))
    is_real = lax.broadcasted_iota(jnp.int32, (kept, 2 * CELL * CELL), 1) // CELL % 2 == 0
    spectrum = jnp.where(is_real, both[:kept], both[kept:])
    for r in range(n):
        send1[r] = spectrum[r * nf : (r + 1) * nf]

    def exchange(source, target, send_sem, recv_sem):
        @pl.loop(1, n)
        def _(step):
            peer, where = coords(step)
            pltpu.make_async_remote_copy(
                src_ref=source.at[peer],
                dst_ref=target.at[rank],
                send_sem=send_sem,
                recv_sem=recv_sem,
                device_id=where,
                device_id_type=MESH,
            ).start()

        target[rank] = source[rank]
        others = pl.ds(0, n - 1)
        pltpu.make_async_copy(source.at[others], source.at[others], send_sem).wait()
        pltpu.make_async_copy(target.at[others], target.at[others], recv_sem).wait()

    exchange(send1, recv1, send_sem1, recv_sem1)

    for ay in range(n_py):
        for t in range(n_pz // GROUPS):
            tiles = [recv1[ay * n_pz + t * GROUPS + g] for g in range(GROUPS)]
            for a, tile in enumerate(swap_groups(tiles)):
                start = (ay * CELL + a) * nf
                field[start : start + nf, t * 128 : (t + 1) * 128] = tile
    width = 2 * CELL * n_pz

    def plane_transform(values, table):
        count = table.shape[0]
        along = dot_parts(split(values, count), [table[i] for i in range(count)])
        joined = jnp.concatenate([along[:, :width], along[:, width:]], axis=0)
        return dot_parts([rows[i] for i in range(count)], split(joined, count))

    values = field[...]
    row = lax.broadcasted_iota(jnp.int32, values.shape, 0)
    col = lax.broadcasted_iota(jnp.int32, values.shape, 1)
    constant = (row % nf + rank * nf == 0) & (col // CELL % 2 == 0)
    mean = jnp.sum(jnp.where(constant, values, 0.0), axis=0, keepdims=True)
    mean = jnp.sum(mean, axis=1, keepdims=True) * (1.0 / (CELL * CELL * n))
    values = values - jnp.where(constant, mean, 0.0)
    solved = plane_transform(plane_transform(values, fwd) * green, inv)
    for ay in range(n_py):
        for t in range(n_pz // GROUPS):
            tiles = []
            for a in range(CELL):
                start = (ay * CELL + a) * nf
                tiles.append(solved[start : start + nf, t * 128 : (t + 1) * 128])
            for g, tile in enumerate(swap_groups(tiles)):
                send2[ay * n_pz + t * GROUPS + g] = tile

    exchange(send2, recv2, send_sem2, recv_sem2)

    for r in range(n):
        waves[r * nf : (r + 1) * nf] = recv2[r]
    columns = split(jnp.transpose(waves[...]), 3)
    cosines = dot_parts(columns, [line[i, :kept] for i in range(3)])
    sines = dot_parts(columns, [line[i, kept:] for i in range(3)])
    potential = [
        cosines[a * PAIR : a * PAIR + CELL] + sines[a * PAIR + CELL : (a + 1) * PAIR]
        for a in range(CELL)
    ]
    edge_out[0] = potential[CELL - 1]
    edge_out[1] = potential[0]
    edge_out[2] = jnp.concatenate([tile[CELL - 1 : CELL] for tile in potential], axis=0)
    edge_out[3] = jnp.concatenate([tile[0:1] for tile in potential], axis=0)
    edges = [
        pltpu.make_async_remote_copy(
            src_ref=edge_out.at[i],
            dst_ref=edge_in.at[i],
            send_sem=edge_send.at[i],
            recv_sem=edge_recv.at[i],
            device_id=target,
            device_id_type=MESH,
        )
        for i, target in enumerate(
            [(up_y, my_z), (down_y, my_z), (my_y, up_z), (my_y, down_z)]
        )
    ]
    for edge in edges:
        edge.start()
    for a, tile in enumerate(potential):
        out_ref[2, a] = (pltpu.roll(tile, 1, 1) - pltpu.roll(tile, nx - 1, 1)) * 0.5
    for edge in edges:
        edge.wait()
    before, after = edge_in[2], edge_in[3]
    lane_row = lax.broadcasted_iota(jnp.int32, (CELL, nx), 0)
    for a, tile in enumerate(potential):
        below = potential[a - 1] if a else edge_in[0]
        above = potential[a + 1] if a < CELL - 1 else edge_in[1]
        out_ref[0, a] = (below - above) * 0.5
        lower = jnp.where(lane_row == 0, before[a : a + 1], pltpu.roll(tile, 1, 0))
        upper = jnp.where(lane_row == CELL - 1, after[a : a + 1], pltpu.roll(tile, CELL - 1, 0))
        out_ref[1, a] = (lower - upper) * 0.5


def solution(mesh):
    n_py, n_pz = mesh.shape["py"], mesh.shape["pz"]
    n = n_py * n_pz
    nx = 512
    nf = nx // 2 // n
    ny, nz = CELL * n_py, CELL * n_pz
    consts = tables(n_py, n_pz, nx, nf)

    def shards(positions, masses):
        chunk = min(positions.shape[1], 2048)
        vmem = pl.BlockSpec(memory_space=pltpu.VMEM)
        hbm = pl.BlockSpec(memory_space=pltpu.HBM)
        block = pltpu.VMEM((n, nf, 128), F32)
        dma = pltpu.SemaphoreType.DMA
        return pl.pallas_call(
            functools.partial(kernel, n_py, n_pz, nx, nf, chunk),
            out_shape=jax.ShapeDtypeStruct((3, CELL, CELL, nx), F32),
            in_specs=[hbm] * 6,
            out_specs=vmem,
            scratch_shapes=[
                pltpu.VMEM(positions.shape, F32),
                pltpu.VMEM((1, positions.shape[1]), F32),
                *[pltpu.VMEM(table.shape, BF16) for table in consts],
                dma((6,)),
                pltpu.VMEM((nx, positions.shape[1]), BF16),
                pltpu.VMEM((4 * 3 * CELL, nx), F32),
                pltpu.VMEM((4 * CELL * CELL, nx), F32),
                pltpu.VMEM((3, CELL, nx), F32),
                pltpu.VMEM((3, CELL, nx), F32),
                dma((3,)),
                dma((3,)),
                block,
                block,
                pltpu.VMEM((ny * nf, 2 * nz), F32),
                block,
                block,
                pltpu.VMEM((n * nf, 128), F32),
                dma, dma, dma, dma,
                pltpu.VMEM((4, CELL, nx), F32),
                pltpu.VMEM((4, CELL, nx), F32),
                dma((4,)),
                dma((4,)),
            ],
            compiler_params=pltpu.CompilerParams(
                collective_id=0, has_side_effects=True, vmem_limit_bytes=67_043_328
            ),
        )(positions, masses.reshape(1, -1), *[jnp.asarray(table) for table in consts])

    return jax.shard_map(
        shards,
        mesh=mesh,
        in_specs=(P(None, ("py", "pz")), P(("py", "pz"))),
        out_specs=P(None, "py", "pz", None),
        check_vma=False,
    )
```

profile of v0, /device:TPU:0, one launch (start us, length us, event | category | flops | bytes accessed | tf_op | source)
XLA Modules:
  0.0 30.3 jit_solution(3683883781473046811)
XLA Ops:
  0.0 28.5 %shard_map.64 = f32[3,8,8,512]{3,2,1,0:T(8,128)} custom-call(f32[3,4096]{1,0:T(4,128)} %pos_hbm.1, f32[1,4096]{1,0:T(1,128)} %bitcast.1, bf16[3,512,512]{2,1,0:T(8,128)(2,1)} %constant.8.clone.line_hbm, bf16[3,256,512]{2,1,0:T(8,128)(2,1)} %constant.9.clone.rows_hbm, bf16[2,128,256]{2,1,0:T(8,128)(2,1)} %constant.10.clone.fwd_hbm, ...), custom_call_target="tpu_custom_call" | custom-call | tf_op jit(solution)/shard_map/pallas_call | solution.py:374
  28.5 1.8 %copy.8 = f32[3,8,8,512]{3,2,1,0:T(8,128)} copy(f32[3,8,8,512]{3,2,1,0:T(8,128)} %shard_map.64) | data formatting | bytes 786432
where the time goes:
time: 30.5 us; the launch traced here: 30.3 us
  Pallas kernels  28.5 us (93%)
  local copies, waits for them, and re-layouts  1.77 us (6%)
    pallas_call x1, Pallas kernels, shards(): pl.pallas_call(functools.partial(kernel, n_py, n_pz, nx, nf, chunk), out_...  28.5 us
    unnamed x1, local copies, waits for them, and re-layouts  1.77 us

commit v1 on v0

--- a/solution.py
+++ b/solution.py
@@ -114,7 +114,7 @@
 def kernel(
     n_py, n_pz, nx, nf, chunk,
     pos_hbm, mass_hbm, line_hbm, rows_hbm, fwd_hbm, inv_hbm,
-    out_ref,
+    pot_ref, side_ref,
     pos_ref, mass_ref, line, rows, fwd, inv, table_sem,
     hot, acc_halo, acc, halo_out, halo_in, halo_send, halo_recv,
     send1, recv1, field, send2, recv2, waves,
@@ -343,18 +343,39 @@
     for edge in edges:
         edge.start()
     for a, tile in enumerate(potential):
-        out_ref[2, a] = (pltpu.roll(tile, 1, 1) - pltpu.roll(tile, nx - 1, 1)) * 0.5
+        pot_ref[a] = tile
     for edge in edges:
         edge.wait()
-    before, after = edge_in[2], edge_in[3]
+    side_ref[...] = edge_in[...]
+
+
+def finish(pot_ref, side_ref, out_hbm, out_ref, sems):
+    nx = pot_ref.shape[2]
+    copies = []
+
+    def emit(d):
+        copies.append(pltpu.make_async_copy(out_ref.at[d], out_hbm.at[d], sems.at[d]))
+        copies[-1].start()
+
+    for a in range(CELL):
+        tile = pot_ref[a]
+        out_ref[2, a] = (pltpu.roll(tile, 1, 1) - pltpu.roll(tile, nx - 1, 1)) * 0.5
+    emit(2)
+    for a in range(CELL):
+        below = pot_ref[a - 1] if a else side_ref[0]
+        above = pot_ref[a + 1] if a < CELL - 1 else side_ref[1]
+        out_ref[0, a] = (below - above) * 0.5
+    emit(0)
+    before, after = side_ref[2], side_ref[3]
     lane_row = lax.broadcasted_iota(jnp.int32, (CELL, nx), 0)
-    for a, tile in enumerate(potential):
-        below = potential[a - 1] if a else edge_in[0]
-        above = potential[a + 1] if a < CELL - 1 else edge_in[1]
-        out_ref[0, a] = (below - above) * 0.5
+    for a in range(CELL):
+        tile = pot_ref[a]
         lower = jnp.where(lane_row == 0, before[a : a + 1], pltpu.roll(tile, 1, 0))
         upper = jnp.where(lane_row == CELL - 1, after[a : a + 1], pltpu.roll(tile, CELL - 1, 0))
         out_ref[1, a] = (lower - upper) * 0.5
+    emit(1)
+    for copy in copies:
+        copy.wait()
 
 
 def solution(mesh):
@@ -371,11 +392,11 @@
         hbm = pl.BlockSpec(memory_space=pltpu.HBM)
         block = pltpu.VMEM((n, nf, 128), F32)
         dma = pltpu.SemaphoreType.DMA
-        return pl.pallas_call(
+        pot, side = pl.pallas_call(
             functools.partial(kernel, n_py, n_pz, nx, nf, chunk),
-            out_shape=jax.ShapeDtypeStruct((3, CELL, CELL, nx), F32),
+            out_shape=[pltpu.VMEM((CELL, CELL, nx), F32), pltpu.VMEM((4, CELL, nx), F32)],
             in_specs=[hbm] * 6,
-            out_specs=vmem,
+            out_specs=[vmem, vmem],
             scratch_shapes=[
                 pltpu.VMEM(positions.shape, F32),
                 pltpu.VMEM((1, positions.shape[1]), F32),
@@ -401,9 +422,20 @@
                 dma((4,)),
             ],
             compiler_params=pltpu.CompilerParams(
-                collective_id=0, has_side_effects=True, vmem_limit_bytes=67_043_328
+                collective_id=0, has_side_effects=True, vmem_limit_bytes=50 << 20
             ),
-        )(positions, masses.reshape(1, -1), *[jnp.asarray(table) for table in consts])
+        )(*[
+            pltpu.with_memory_space_constraint(x, pltpu.HBM)
+            for x in (positions, masses.reshape(1, -1), *map(jnp.asarray, consts))
+        ])
+        return pl.pallas_call(
+            finish,
+            out_shape=jax.ShapeDtypeStruct((3, CELL, CELL, nx), F32),
+            in_specs=[vmem, vmem],
+            out_specs=hbm,
+            scratch_shapes=[pltpu.VMEM((3, CELL, CELL, nx), F32), dma((3,))],
+            compiler_params=pltpu.CompilerParams(vmem_limit_bytes=16 << 20),
+        )(pot, side)
 
     return jax.shard_map(
         shards,

time: 30.5 us -> 28.8 us (0.944)
  local copies, waits for them, and re-layouts: 1.77 us -> 0 us
    unnamed x1 -> x0, local copies, waits for them, and re-layouts: 1.77 us -> none
    pallas_call x0 -> x1, Pallas kernels: none -> 0.91 us  [shards(): pl.pallas_call(finish, out_shape=jax.ShapeDtypeStruct((3, CELL, CELL, nx)...]
    pallas_call x1, Pallas kernels: 28.5 us -> 27.7 us  [shards(): pl.pallas_call(functools.partial(kernel, n_py, n_pz, nx, nf, chunk), out_...]
where the time goes in v1:
time: 28.8 us; the launch traced here: 28.7 us
  Pallas kernels  28.6 us (99%)
    pallas_call x1, Pallas kernels, shards(): pl.pallas_call(functools.partial(kernel, n_py, n_pz, nx, nf, chunk), out_...  27.7 us
    pallas_call x1, Pallas kernels, shards(): pl.pallas_call(finish, out_shape=jax.ShapeDtypeStruct((3, CELL, CELL, nx)...  0.91 us

profile of v1, /device:TPU:0, one launch (start us, length us, event | category | flops | bytes accessed | tf_op | source)
XLA Modules:
  0.0 28.7 jit_solution(14174861911467914001)
XLA Ops:
  0.0 27.7 %shard_map.64 = (f32[8,8,512]{2,1,0:T(8,128)S(1)}, f32[4,8,512]{2,1,0:T(8,128)S(1)}) custom-call(f32[3,4096]{1,0:T(4,128)} %pos_hbm.1, f32[1,4096]{1,0:T(1,128)} %bitcast.1, bf16[3,512,512]{2,1,0:T(8,128)(2,1)} %constant.8.clone.line_hbm, bf16[3,256,512]{2,1,0:T(8,128)(2,1)} %constant.9.clone.rows_hbm, bf16[2,128,256]{2,1,0:T(8,128)(2,1)} %constant.10.clone.fwd_hbm, ...), custom_call_target="tpu_custom_call" | custom-call | tf_op jit(solution)/shard_map/pallas_call | solution.py:395
  27.7 0.9 %shard_map.65 = f32[3,8,8,512]{3,2,1,0:T(8,128)} custom-call(f32[8,8,512]{2,1,0:T(8,128)S(1)} %get-tuple-element.7.pot_ref, f32[4,8,512]{2,1,0:T(8,128)S(1)} %get-tuple-element.8.side_ref), custom_call_target="tpu_custom_call" | custom-call | tf_op jit(solution)/shard_map/pallas_call | solution.py:431

commit v2 on v1

v2 whole, which is shorter than its diff:
```python
import functools
import math

import jax
import jax.numpy as jnp
import ml_dtypes
import numpy as np
from jax import lax
from jax.experimental import pallas as pl
from jax.experimental.pallas import tpu as pltpu
from jax.sharding import PartitionSpec as P

MESH = pl.DeviceIdType.MESH
F32 = jnp.float32
BF16 = jnp.bfloat16
SMOOTHING_SQ = 0.25
CELL = 8
CELLS = CELL * CELL
EDGE = 32


def parts(table, count):
    out = []
    for _ in range(count):
        out.append(table.astype(ml_dtypes.bfloat16))
        table = table - out[-1].astype(np.float64)
    return np.stack(out)


def real_form(wave, turned):
    wave = wave * 1j if turned else wave
    return np.block([[wave.real, wave.imag], [-wave.imag, wave.real]])


def tables(n_py, n_pz, nx, nf):
    n = n_py * n_pz
    ny, nz = CELL * n_py, CELL * n_pz
    quarter, half_nf = nx // 4, nf // 2
    along = (2 * np.arange(quarter)[None, :] + np.arange(2)[:, None]).reshape(-1)
    order = np.arange(quarter).reshape(n // 2, 2, half_nf).transpose(1, 0, 2).reshape(-1)
    line, back = [], []
    for odd in range(2):
        waves = 2 * np.arange(quarter) + odd
        phase = (np.outer(waves, along) % nx) * (2 * np.pi / nx)
        line.append(parts(np.concatenate([np.cos(phase), -np.sin(phase)]), 2))
        phase = (np.outer(waves[order], np.arange(nx // 2)) % nx) * (2 * np.pi / nx)
        back.append(parts(np.concatenate([np.cos(phase), -np.sin(phase)]), 3))

    inner = [(a, z) for a in range(CELL) for z in range(CELL)]
    upper = [(CELL, z) for z in range(CELL)] + [(a, CELL) for a in range(CELL)] + [(CELL, CELL)]
    outer = [(-1, z) for z in range(CELL)] + [(CELL, z) for z in range(CELL)]
    outer += [(a, -1) for a in range(CELL)] + [(a, CELL) for a in range(CELL)]
    used = np.zeros(EDGE)
    used[: len(upper)] = 1.0
    upper = np.array(upper + [(0, 0)] * (EDGE - len(upper)))
    inner, outer = np.array(inner), np.array(outer)

    def inside(cells, sign):
        return np.exp(sign * 2j * np.pi * (cells @ np.array(inner).T) / CELL)

    def twiddles(cells, copies):
        p = np.arange(n)
        phase = 2 * np.pi * (
            np.outer(p // n_pz, cells[:, 0]) / ny + np.outer(p % n_pz, cells[:, 1]) / nz
        )
        return np.tile(np.stack([np.cos(phase), np.sin(phase)]), (1, 1, copies))

    share = lambda at: np.where((at == 0) | (at == CELL), 0.5, 1.0)
    flat = share(inner[:, 0]) * share(inner[:, 1])
    flat_edge = share(upper[:, 0]) * share(upper[:, 1]) * used
    pattern = np.zeros((CELL, 256))
    pattern[0, :CELLS] = flat
    pattern[0, 128 : 128 + EDGE] = flat_edge
    turn = np.concatenate([twiddles(inner, 2), twiddles(upper, 4)], axis=2).reshape(2 * n, 256)
    turn = np.concatenate([turn, pattern]).astype(np.float32)
    unturn = np.concatenate([twiddles(inner, 2), twiddles(outer, 4)], axis=2)
    unturn = unturn.reshape(2 * n, 256).astype(np.float32)

    wave = inside(inner, -1)
    fwd = parts(np.concatenate([real_form(wave, 0), real_form(wave, 1)]), 2)
    fwd = np.concatenate([fwd[0], fwd[1]], axis=1)
    wave = inside(upper, -1) * used[:, None]
    spread = [np.kron(np.eye(2), real_form(wave, t)) for t in range(2)]
    fwd_edge = parts(np.concatenate(spread), 2)
    wave, wave_edge = inside(inner, 1).T, inside(outer, 1).T
    pieces = [real_form(wave, 0), real_form(wave, 1)]
    pieces += [np.tile(real_form(wave_edge, t), (1, 2)) for t in range(2)]
    inv = parts(np.concatenate(pieces, axis=1), 2)
    inv = np.concatenate([inv[0], inv[0], inv[1]])
    return np.stack(line), np.stack(back), fwd, fwd_edge, inv, turn, unturn


def plus(a, b):
    return b if a is None else a if b is None else a + b


def minus(a, b):
    return a if b is None else -b if a is None else a - b


def conj(x):
    return x[0], minus(None, x[1]) if x[1] is not None else None


def add(x, y):
    return plus(x[0], y[0]), plus(x[1], y[1])


def sub(x, y):
    return minus(x[0], y[0]), minus(x[1], y[1])


def rotated(x, k, n, sign):
    re, im = x
    if k == 0:
        return x
    if 4 * k == n:
        turned = (minus(None, im) if im is not None else None, re)
        return turned if sign > 0 else (im, -re)
    c, s = math.cos(2 * math.pi * k / n), sign * math.sin(2 * math.pi * k / n)
    if im is None:
        return re * c, re * s
    if 8 * k == n:
        both = (re - im, re + im) if sign > 0 else (re + im, im - re)
        return both[0] * c, both[1] * c
    return re * c - im * s, re * s + im * c


def fft(x, sign):
    n = len(x)
    if n == 1:
        return x
    even, odd = fft(x[::2], sign), fft(x[1::2], sign)
    odd = [rotated(o, k, n, sign) for k, o in enumerate(odd)]
    return [add(e, o) for e, o in zip(even, odd)] + [sub(e, o) for e, o in zip(even, odd)]


def rfft(x):
    n = len(x)
    if n == 1:
        return [(x[0], None)]
    if n == 2:
        return [(x[0] + x[1], None), (x[0] - x[1], None)]
    even, odd = rfft(x[::2]), rfft(x[1::2])
    out = [None] * (n // 2 + 1)
    for k in range(n // 4 + 1):
        turned = rotated(odd[k], k, n, -1)
        out[k] = add(even[k], turned)
        if k < n // 4:
            out[n // 2 - k] = conj(sub(even[k], turned))
    return out


def irfft(x):
    n = 2 * (len(x) - 1)
    if n == 2:
        return [x[0][0] + x[1][0], x[0][0] - x[1][0]]
    even, odd = [], []
    for k in range(n // 4 + 1):
        if 4 * k == n:
            even.append((x[k][0] * 2.0, None))
            odd.append((x[k][1] * -2.0, None) if x[k][1] is not None else (x[k][0] * 0.0, None))
            continue
        mirror = conj(x[n // 2 - k])
        even.append(add(x[k], mirror))
        odd.append(rotated(sub(x[k], mirror), k, n, 1))
    even, odd = irfft(even), irfft(odd)
    return [v for pair in zip(even, odd) for v in pair]


def plane_forward(values, n_py, n_pz):
    lines = [rfft(row) for row in values]
    out = {}
    for pz in range(n_pz // 2 + 1):
        column = [line[pz] for line in lines]
        if all(x[1] is None for x in column):
            found = rfft([x[0] for x in column])
            found += [conj(found[n_py - py]) for py in range(n_py // 2 + 1, n_py)]
        else:
            found = fft(column, -1)
        for py in range(n_py):
            out[py, pz] = found[py]
    return out


def plane_inverse(half, n_py, n_pz):
    columns = []
    for pz in range(n_pz // 2 + 1):
        if pz in (0, n_pz // 2):
            column = irfft([half[py, pz] for py in range(n_py // 2 + 1)])
            columns.append([(x, None) for x in column])
        else:
            columns.append(fft([half[py, pz] for py in range(n_py)], 1))
    return [irfft([column[ay] for column in columns]) for ay in range(n_py)]


def split(x, count=2):
    out = []
    for i in range(count):
        out.append(x.astype(BF16))
        if i < count - 1:
            x = x - out[-1].astype(F32)
    return out


def dot(left, right, dims=((1,), (0,))):
    return lax.dot_general(left, right, (dims, ((), ())), preferred_element_type=F32)


def dot_parts(left, right, dims=((1,), (0,))):
    count = len(left)
    total = None
    for order in reversed(range(count)):
        for i in range(order + 1):
            term = dot(left[i], right[order - i], dims)
            total = term if total is None else total + term
    return total


def green_factor(rank, n_py, n_pz, nx, nf):
    n = n_py * n_pz
    ny, nz = CELL * n_py, CELL * n_pz
    shape = (n * nf, 128)
    row = lax.broadcasted_iota(jnp.int32, shape, 0)
    col = lax.broadcasted_iota(jnp.int32, shape, 1)

    def square(wave, period):
        folded = jnp.minimum(wave, period - wave).astype(F32)
        return (folded * (2.0 * math.pi / period)) ** 2

    p = row // nf
    wave_x = 2 * (lax.rem(rank, n // 2) * nf + row % nf) + rank // (n // 2)
    wave_y = p // n_pz + n_py * (col // CELL % CELL)
    wave_z = p % n_pz + n_pz * (col % CELL)
    total = square(wave_y, ny) + square(wave_z, nz) + square(wave_x, nx)
    safe = jnp.where(total > 0, total, 1.0)
    green = jnp.where(total > 0, -4.0 * math.pi * jnp.exp(-SMOOTHING_SQ * total) / safe, 0.0)
    return green * (jnp.where(wave_x > 0, 1.0, 0.5) * (1.0 / float(ny * nz * nx)))


def kernel(
    n_py, n_pz, nx, nf, chunk,
    pos_hbm, mass_hbm, line_hbm, back_hbm, fwd_hbm, fwd_edge_hbm, inv_hbm, turn_hbm, unturn_hbm,
    pot_ref, side_ref,
    pos_ref, mass_ref, line, back, fwd, fwd_edge, inv, turn, unturn, table_sem,
    acc, green, mixed, send1, recv1, send2, recv2, send_edge, recv_edge, waves_edge,
    send_sem1, recv_sem1, send_sem2, recv_sem2, send_sem3, recv_sem3,
):
    n = n_py * n_pz
    half_nf, half, quarter = nf // 2, nx // 2, nx // 4
    my_y, my_z = lax.axis_index("py"), lax.axis_index("pz")
    rank = my_y * n_pz + my_z

    loads = [
        pltpu.make_async_copy(src, dst, table_sem.at[i])
        for i, (src, dst) in enumerate(
            [
                (pos_hbm, pos_ref),
                (mass_hbm, mass_ref),
                (line_hbm, line),
                (turn_hbm, turn),
                (fwd_hbm, fwd),
                (fwd_edge_hbm, fwd_edge),
                (inv_hbm, inv),
                (unturn_hbm, unturn),
                (back_hbm, back),
            ]
        )
    ]
    for load in loads:
        load.start()

    def coords(step):
        along_z = (n - step) // n_py
        along_z = along_z ^ (2 * (along_z // 4))
        other_y = lax.rem(n - step, n_py) ^ my_y
        other_z = along_z ^ my_z
        return other_y * n_pz + other_z, (other_y, other_z)

    barrier = pltpu.get_barrier_semaphore()

    @pl.loop(1, n)
    def _(step):
        pl.semaphore_signal(barrier, inc=1, device_id=coords(step)[1], device_id_type=MESH)

    base_y = (my_y * CELL).astype(F32)
    base_z = (my_z * CELL).astype(F32)
    row_of = lax.broadcasted_iota(jnp.int32, (CELL, chunk), 0)
    cell = row_of.astype(F32)
    sublane = lax.broadcasted_iota(jnp.int32, (2 * CELL, chunk), 0).astype(F32)

    for load in loads[:2]:
        load.wait()

    def deposited(turn_index):
        span = pl.ds(pl.multiple_of(turn_index * chunk, chunk), chunk)
        along_y = pos_ref[0:1, span] - base_y
        along_z = pos_ref[1:2, span] - base_z
        along_x = pos_ref[2:3, span]
        mass = mass_ref[0:1, span]
        floor_x = jnp.floor(along_x)
        frac_x = along_x - floor_x
        pair = jnp.floor(floor_x * 0.5)
        is_even = floor_x == 2.0 * pair
        lower, upper = mass * (1.0 - frac_x), mass * frac_x
        shares = [
            jnp.where(is_even, lower, 0.0),
            jnp.where(is_even, upper, lower),
            jnp.where(is_even, 0.0, upper),
        ]
        where_x = jnp.broadcast_to(pair, (2 * CELL, chunk)).astype(BF16)
        one_hot = jnp.concatenate(
            [
                jnp.where(
                    where_x == (sublane + float(t)).astype(BF16),
                    jnp.ones((), BF16),
                    jnp.zeros((), BF16),
                )
                for t in range(0, half, 2 * CELL)
            ],
            axis=0,
        )
        hat_y = jnp.maximum(1.0 - jnp.abs(along_y - cell), 0.0)
        hat_z = jnp.maximum(1.0 - jnp.abs(along_z - cell), 0.0)
        last_y = jnp.maximum(along_y - (CELL - 1.0), 0.0)
        last_z = jnp.maximum(along_z - (CELL - 1.0), 0.0)
        tiles = []
        for share in shares:
            scaled = hat_z * share
            tiles += [hat_y[a : a + 1] * scaled for a in range(CELL)]
            tiles += [last_y * scaled, hat_y * (last_z * share)]
        corner = jnp.where(row_of == 0, shares[0], jnp.where(row_of == 1, shares[1], shares[2]))
        tiles.append(jnp.where(row_of < 3, corner * (last_y * last_z), 0.0))
        pair_of = split(jnp.concatenate(tiles, axis=0))
        return dot(jnp.concatenate(pair_of, axis=0), one_hot, ((1,), (1,)))

    turns = pos_ref.shape[1] // chunk
    acc[...] = deposited(0)
    if turns > 1:

        @pl.loop(1, turns)
        def _(turn_index):
            acc[...] += deposited(turn_index)

    for load in loads[2:3]:
        load.wait()
    sums = acc[...]
    rows = sums.shape[0] // 2
    sums = sums[:rows] + sums[rows:]
    block = CELLS + 2 * CELL
    even = sums[:block] + pltpu.roll(sums[2 * block : 3 * block], 1, 1)
    odd = sums[block : 2 * block]
    corner = sums[3 * block :]
    first = lax.broadcasted_iota(jnp.int32, (CELL, half), 0) == 0
    blank = jnp.zeros((CELL, half), F32)
    corner_even = corner + pltpu.roll(pltpu.roll(corner, CELL - 2, 0), 1, 1)
    corner_even = jnp.where(first, corner_even, 0.0)
    corner_odd = jnp.where(first, pltpu.roll(corner, CELL - 1, 0), 0.0)
    even = jnp.concatenate([even, corner_even, blank], axis=0)
    odd = jnp.concatenate([odd, corner_odd, blank], axis=0)

    lane = lax.broadcasted_iota(jnp.int32, (nf, 128), 1)
    is_real = lane < CELLS
    is_real_edge = lane % CELLS < EDGE
    low_half = lax.broadcasted_iota(jnp.int32, (half_nf, 128), 1) < CELLS
    for parity in range(2):
        folded = []
        for grid in (even, odd):
            left, right = grid[:, :quarter], grid[:, quarter:]
            folded.append(left - right if parity else left + right)
        density = [
            jnp.concatenate([x[:CELLS]] * 2 + [x[CELLS:]] * 4, axis=0)
            for x in split(jnp.concatenate(folded, axis=1))
        ]
        both = dot_parts([line[parity, 0], line[parity, 1]], density, ((1,), (1,)))
        for r in range(n // 2):
            re, im = both[r * nf : (r + 1) * nf], both[quarter + r * nf : quarter + (r + 1) * nf]
            peer = parity * (n // 2) + r
            send1[peer, 0:nf] = jnp.where(is_real, re[:, :128], im[:, :128])
            side = jnp.where(is_real_edge, re[:, 128:], im[:, 128:])
            send1[peer, nf : nf + half_nf] = jnp.where(low_half, side[:half_nf], side[half_nf:])

    pl.semaphore_wait(barrier, n - 1)

    def start(source, target, send_sem, recv_sem):
        @pl.loop(1, n)
        def _(step):
            peer, where = coords(step)
            pltpu.make_async_remote_copy(
                src_ref=source.at[peer],
                dst_ref=target.at[rank],
                send_sem=send_sem,
                recv_sem=recv_sem,
                device_id=where,
                device_id_type=MESH,
            ).start()

        target[rank] = source[rank]

    def finish_exchange(source, target, send_sem, recv_sem):
        others = pl.ds(0, n - 1)
        pltpu.make_async_copy(target.at[others], target.at[others], recv_sem).wait()
        pltpu.make_async_copy(source.at[others], source.at[others], send_sem).wait()

    with jax.named_scope("exch1"):
        start(send1, recv1, send_sem1, recv_sem1)
        green[...] = green_factor(rank, n_py, n_pz, nx, nf)
        for load in loads[3:]:
            load.wait()
        with jax.named_scope("wait1"):
            finish_exchange(send1, recv1, send_sem1, recv_sem1)

    def at(ref, row):
        return ref[row : row + 1]

    def every(half_plane, py, pz):
        if pz <= n_pz // 2:
            return half_plane[py, pz], 1
        return half_plane[-py % n_py, n_pz - pz], -1

    turned = []
    for lanes, span, height in (
        (slice(0, 128), slice(0, nf), nf),
        (slice(128, 256), slice(nf, nf + half_nf), half_nf),
    ):
        values = [[recv1[ay * n_pz + az, span] for az in range(n_pz)] for ay in range(n_py)]
        found = plane_forward(values, n_py, n_pz)
        blocks = []
        for p in range(n):
            (re, im), sign = every(found, p // n_pz, p % n_pz)
            c, s = turn[p : p + 1, lanes], turn[n + p : n + p + 1, lanes]
            if im is None:
                u, v = c * re, -(s * re)
            elif sign > 0:
                u, v = c * re + s * im, c * im - s * re
            else:
                u, v = c * re - s * im, -(c * im) - s * re
            blocks.append([u, v])
        turned.append(blocks)
    corner_row = lax.broadcasted_iota(jnp.int32, (half_nf, 128), 0) == 0
    top_row = lax.broadcasted_iota(jnp.int32, (nf, 128), 0) == 0
    level = jnp.sum(turned[0][0][0][0:1] * jnp.where(is_real[0:1], 1.0, 0.0), axis=1, keepdims=True)
    level += jnp.sum(
        turned[1][0][0][0:1] * jnp.where(lane[0:1] < EDGE, 1.0, 0.0), axis=1, keepdims=True
    )
    level = jnp.where(rank == 0, level * (1.0 / CELLS), 0.0)
    flat = turn[2 * n : 2 * n + 1]
    turned[0][0][0] = turned[0][0][0] - jnp.where(top_row, level * flat[:, :128], 0.0)
    turned[1][0][0] = turned[1][0][0] - jnp.where(corner_row, level * flat[:, 128:], 0.0)

    stacked = [
        jnp.concatenate(
            [jnp.concatenate([uv[i] for uv in blocks], axis=0) for i in range(2)], axis=1
        )
        for blocks in turned
    ]
    high, low = split(stacked[0])
    wide = dot(high, fwd[...])
    solved = wide[:, :128] + wide[:, 128:] + dot(low, fwd[:, :128])
    beside = dot_parts(split(stacked[1]), [fwd_edge[0], fwd_edge[1]])
    pieces = []
    for p in range(n):
        rows_of = beside[p * half_nf : (p + 1) * half_nf]
        pieces += [rows_of[:, :128], rows_of[:, 128:]]
    solved = (solved + jnp.concatenate(pieces, axis=0)) * green[...]
    high, low = split(solved)
    mixed[...] = dot(jnp.concatenate([high, low], axis=1), inv[0:256]) + dot(high, inv[256:384])

    for lanes, offset in ((slice(0, 128), 0), (slice(128, 256), 256)):
        ones, twos = {}, {}
        for p in range(n):
            c, s = unturn[p : p + 1, lanes], unturn[n + p : n + p + 1, lanes]
            span = slice(p * nf, (p + 1) * nf)
            y, jy = mixed[span, offset : offset + 128], mixed[span, offset + 128 : offset + 256]
            ones[p // n_pz, p % n_pz] = c * y + s * jy
            twos[p // n_pz, p % n_pz] = c * jy - s * y
        half_plane = {}
        for pz in range(n_pz // 2 + 1):
            for py in range(n_py):
                other = (-py % n_py, -pz % n_pz)
                if other == (py, pz):
                    half_plane[py, pz] = (ones[other] * 2.0, None)
                else:
                    half_plane[py, pz] = (
                        ones[py, pz] + ones[other],
                        twos[other] - twos[py, pz],
                    )
        values = plane_inverse(half_plane, n_py, n_pz)
        for ay in range(n_py):
            for az in range(n_pz):
                value = values[ay][az]
                if offset == 0:
                    send2[ay * n_pz + az] = value
                else:
                    value = jnp.where(low_half, value[:half_nf], value[half_nf:])
                    send_edge[ay * n_pz + az] = value
        if offset == 0:
            start(send2, recv2, send_sem2, recv_sem2)
        else:
            start(send_edge, recv_edge, send_sem3, recv_sem3)

    with jax.named_scope("wait2"):
        finish_exchange(send2, recv2, send_sem2, recv_sem2)

    def potential(columns):
        found = [
            dot_parts(split(columns[parity], 3), [back[parity, i] for i in range(3)])
            for parity in range(2)
        ]
        return found[0] + found[1], found[0] - found[1]

    columns = []
    for parity in range(2):
        peers = range(parity * (n // 2), (parity + 1) * (n // 2))
        rows_of = [
            recv2[r, h * half_nf : (h + 1) * half_nf] for h in range(2) for r in peers
        ]
        turned_back = jnp.transpose(jnp.concatenate(rows_of, axis=0))
        columns.append(jnp.concatenate([turned_back[:CELLS], turned_back[CELLS:]], axis=1))
    left, right = potential(columns)
    for a in range(CELL):
        pot_ref[a, :, :half] = left[a * CELL : (a + 1) * CELL]
        pot_ref[a, :, half:] = right[a * CELL : (a + 1) * CELL]

    with jax.named_scope("wait3"):
        finish_exchange(send_edge, recv_edge, send_sem3, recv_sem3)
    for r in range(n):
        waves_edge[r * half_nf : (r + 1) * half_nf] = recv_edge[r]
    turned_back = jnp.transpose(waves_edge[...])
    columns = []
    for parity in range(2):
        span = slice(parity * CELLS, (parity + 1) * CELLS)
        columns.append(
            jnp.concatenate(
                [
                    turned_back[h * CELLS + c * EDGE : h * CELLS + (c + 1) * EDGE, span]
                    for c in range(2)
                    for h in range(2)
                ],
                axis=1,
            )
        )
    left, right = potential(columns)
    for i in range(4):
        side_ref[i, :, :half] = left[i * CELL : (i + 1) * CELL]
        side_ref[i, :, half:] = right[i * CELL : (i + 1) * CELL]


def finish(pot_ref, side_ref, out_hbm, out_ref, sems):
    nx = pot_ref.shape[2]
    copies = []

    def emit(d):
        copies.append(pltpu.make_async_copy(out_ref.at[d], out_hbm.at[d], sems.at[d]))
        copies[-1].start()

    for a in range(CELL):
        tile = pot_ref[a]
        out_ref[2, a] = (pltpu.roll(tile, 1, 1) - pltpu.roll(tile, nx - 1, 1)) * 0.5
    emit(2)
    for a in range(CELL):
        below = pot_ref[a - 1] if a else side_ref[0]
        above = pot_ref[a + 1] if a < CELL - 1 else side_ref[1]
        out_ref[0, a] = (below - above) * 0.5
    emit(0)
    before, after = side_ref[2], side_ref[3]
    lane_row = lax.broadcasted_iota(jnp.int32, (CELL, nx), 0)
    for a in range(CELL):
        tile = pot_ref[a]
        lower = jnp.where(lane_row == 0, before[a : a + 1], pltpu.roll(tile, 1, 0))
        upper = jnp.where(lane_row == CELL - 1, after[a : a + 1], pltpu.roll(tile, CELL - 1, 0))
        out_ref[1, a] = (lower - upper) * 0.5
    emit(1)
    for copy in copies:
        copy.wait()


def solution(mesh):
    n_py, n_pz = mesh.shape["py"], mesh.shape["pz"]
    n = n_py * n_pz
    nx = 512
    nf = nx // 2 // n
    consts = tables(n_py, n_pz, nx, nf)

    def shards(positions, masses):
        chunk = min(positions.shape[1], 2048)
        vmem = pl.BlockSpec(memory_space=pltpu.VMEM)
        hbm = pl.BlockSpec(memory_space=pltpu.HBM)
        dma = pltpu.SemaphoreType.DMA
        wide = pltpu.VMEM((n, nf + nf // 2, 128), F32)
        block = pltpu.VMEM((n, nf, 128), F32)
        edge = pltpu.VMEM((n, nf // 2, 128), F32)
        operands = [positions, masses.reshape(1, -1), *map(jnp.asarray, consts)]
        pot, side = pl.pallas_call(
            functools.partial(kernel, n_py, n_pz, nx, nf, chunk),
            out_shape=[pltpu.VMEM((CELL, CELL, nx), F32), pltpu.VMEM((4, CELL, nx), F32)],
            in_specs=[hbm] * len(operands),
            out_specs=[vmem, vmem],
            scratch_shapes=[
                *[pltpu.VMEM(x.shape, x.dtype) for x in operands],
                dma((len(operands),)),
                pltpu.VMEM((2 * (3 * (CELLS + 2 * CELL) + CELL), nx // 2), F32),
                pltpu.VMEM((n * nf, 128), F32),
                pltpu.VMEM((n * nf, 512), F32),
                wide, wide, block, block, edge, edge,
                pltpu.VMEM((n * nf // 2, 128), F32),
                dma, dma, dma, dma, dma, dma,
            ],
            compiler_params=pltpu.CompilerParams(
                collective_id=0, has_side_effects=True, vmem_limit_bytes=50 << 20
            ),
        )(*[pltpu.with_memory_space_constraint(x, pltpu.HBM) for x in operands])
        return pl.pallas_call(
            finish,
            out_shape=jax.ShapeDtypeStruct((3, CELL, CELL, nx), F32),
            in_specs=[vmem, vmem],
            out_specs=hbm,
            scratch_shapes=[pltpu.VMEM((3, CELL, CELL, nx), F32), dma((3,))],
            compiler_params=pltpu.CompilerParams(vmem_limit_bytes=16 << 20),
        )(pot, side)

    return jax.shard_map(
        shards,
        mesh=mesh,
        in_specs=(P(None, ("py", "pz")), P(("py", "pz"))),
        out_specs=P(None, "py", "pz", None),
        check_vma=False,
    )
```

time: 28.8 us -> 22.7 us (0.79)
  Pallas kernels: 28.6 us -> 22.5 us
    pallas_call x1, Pallas kernels: 27.7 us -> 21.6 us  [shards(): pl.pallas_call(functools.partial(kernel, n_py, n_pz, nx, nf, chunk), out_...]
where the time goes in v2:
time: 22.7 us; the launch traced here: 22.5 us
  Pallas kernels  22.5 us (99%)
    pallas_call x1, Pallas kernels, shards(): pl.pallas_call(functools.partial(kernel, n_py, n_pz, nx, nf, chunk), out_...  21.6 us
    pallas_call x1, Pallas kernels, shards(): pl.pallas_call(finish, out_shape=jax.ShapeDtypeStruct((3, CELL, CELL, nx)...  0.91 us

profile of v2, /device:TPU:0, one launch (start us, length us, event | category | flops | bytes accessed | tf_op | source)
XLA Modules:
  0.0 22.5 jit_solution(10269211432781761053)
XLA Ops:
  0.0 21.6 %shard_map.91 = (f32[8,8,512]{2,1,0:T(8,128)S(1)}, f32[4,8,512]{2,1,0:T(8,128)S(1)}) custom-call(f32[3,4096]{1,0:T(4,128)} %pos_hbm.1, f32[1,4096]{1,0:T(1,128)} %bitcast.1, bf16[2,2,256,256]{3,2,1,0:T(8,128)(2,1)} %constant.14.clone.line_hbm, bf16[2,3,256,256]{3,2,1,0:T(8,128)(2,1)} %constant.15.clone.back_hbm, bf16[256,256]{1,0:T(8,128)(2,1)} %constant.16.clone.fwd_hbm, ...), custom_call_target="tpu_custom_call" | custom-call | tf_op jit(solution)/shard_map/pallas_call | solution.py:594
  21.6 0.9 %shard_map.92 = f32[3,8,8,512]{3,2,1,0:T(8,128)} custom-call(f32[8,8,512]{2,1,0:T(8,128)S(1)} %get-tuple-element.7.pot_ref, f32[4,8,512]{2,1,0:T(8,128)S(1)} %get-tuple-element.8.side_ref), custom_call_target="tpu_custom_call" | custom-call | tf_op jit(solution)/shard_map/pallas_call | solution.py:613

commit v3 on v2

--- a/solution.py
+++ b/solution.py
@@ -217,7 +217,7 @@
     return total
 
 
-def green_factor(rank, n_py, n_pz, nx, nf):
+def green_factor(owner, parity, n_py, n_pz, nx, nf):
     n = n_py * n_pz
     ny, nz = CELL * n_py, CELL * n_pz
     shape = (n * nf, 128)
@@ -229,7 +229,7 @@
         return (folded * (2.0 * math.pi / period)) ** 2
 
     p = row // nf
-    wave_x = 2 * (lax.rem(rank, n // 2) * nf + row % nf) + rank // (n // 2)
+    wave_x = 2 * (owner * nf + row % nf) + parity
     wave_y = p // n_pz + n_py * (col // CELL % CELL)
     wave_z = p % n_pz + n_pz * (col % CELL)
     total = square(wave_y, ny) + square(wave_z, nz) + square(wave_x, nx)
@@ -243,8 +243,8 @@
     pos_hbm, mass_hbm, line_hbm, back_hbm, fwd_hbm, fwd_edge_hbm, inv_hbm, turn_hbm, unturn_hbm,
     pot_ref, side_ref,
     pos_ref, mass_ref, line, back, fwd, fwd_edge, inv, turn, unturn, table_sem,
-    acc, green, mixed, send1, recv1, send2, recv2, send_edge, recv_edge, waves_edge,
-    send_sem1, recv_sem1, send_sem2, recv_sem2, send_sem3, recv_sem3,
+    acc, green, mixed, send1, recv1, send2, recv2, waves_edge,
+    send_sem1, recv_sem1, send_sem2, recv_sem2,
 ):
     n = n_py * n_pz
     half_nf, half, quarter = nf // 2, nx // 2, nx // 4
@@ -267,22 +267,44 @@
             ]
         )
     ]
-    for load in loads:
+    for load in loads[:2]:
         load.start()
 
-    def coords(step):
-        along_z = (n - step) // n_py
-        along_z = along_z ^ (2 * (along_z // 4))
-        other_y = lax.rem(n - step, n_py) ^ my_y
-        other_z = along_z ^ my_z
-        return other_y * n_pz + other_z, (other_y, other_z)
+    n_own, half_z, first_z = n // 2, n_pz // 2, n_pz // 4
+    own_z = my_z - first_z
+    is_owner = (own_z >= 0) & (own_z < half_z)
+    is_guest = jnp.logical_not(is_owner)
+    owner = my_y * half_z + own_z
+    turn_z = jnp.where(my_z >= half_z, first_z, 0) ^ lax.rem(my_z, 2)
+
+    def far_first(step):
+        along = step % n_pz
+        return -(along // 4), -bin(step).count("1"), along % 4 // 2, -step
+
+    everyone, owners = [], []
+    for step in sorted(range(1, n), key=far_first):
+        other_y, other_z = (step // n_pz) ^ my_y, (step % n_pz) ^ my_z
+        everyone.append((other_y * n_pz + other_z, (other_y, other_z)))
+    for step in sorted(range(n_own), key=lambda v: (-(v % half_z // 2), -bin(v // half_z).count("1"))):
+        other_y, other_z = (step // half_z) ^ my_y, (step % half_z) ^ turn_z
+        place = (other_y, other_z + first_z)
+        owners.append((step < half_z, other_y * half_z + other_z, place))
 
     barrier = pltpu.get_barrier_semaphore()
 
-    @pl.loop(1, n)
-    def _(step):
-        pl.semaphore_signal(barrier, inc=1, device_id=coords(step)[1], device_id_type=MESH)
-
+    @pl.when(is_owner)
+    def _():
+        for _, where in everyone:
+            pl.semaphore_signal(barrier, inc=1, device_id=where, device_id_type=MESH)
+
+    @pl.when(is_guest)
+    def _():
+        for _, _, where in owners:
+            pl.semaphore_signal(barrier, inc=1, device_id=where, device_id_type=MESH)
+
+
+    for load in loads[2:]:
+        load.start()
     base_y = (my_y * CELL).astype(F32)
     base_z = (my_z * CELL).astype(F32)
     row_of = lax.broadcasted_iota(jnp.int32, (CELL, chunk), 0)
@@ -294,21 +316,22 @@
 
     def deposited(turn_index):
         span = pl.ds(pl.multiple_of(turn_index * chunk, chunk), chunk)
-        along_y = pos_ref[0:1, span] - base_y
-        along_z = pos_ref[1:2, span] - base_z
-        along_x = pos_ref[2:3, span]
-        mass = mass_ref[0:1, span]
+        tall = (CELL, chunk)
+        along_y = jnp.broadcast_to(pos_ref[0:1, span], tall) - base_y
+        along_z = jnp.broadcast_to(pos_ref[1:2, span], tall) - base_z
+        along_x = jnp.broadcast_to(pos_ref[2:3, span], tall)
+        mass = jnp.broadcast_to(mass_ref[0:1, span], tall)
         floor_x = jnp.floor(along_x)
-        frac_x = along_x - floor_x
-        pair = jnp.floor(floor_x * 0.5)
+        pair = jnp.floor(along_x * 0.5)
         is_even = floor_x == 2.0 * pair
-        lower, upper = mass * (1.0 - frac_x), mass * frac_x
+        upper = mass * (along_x - floor_x)
+        lower = mass * (1.0 - (along_x - floor_x))
         shares = [
             jnp.where(is_even, lower, 0.0),
             jnp.where(is_even, upper, lower),
             jnp.where(is_even, 0.0, upper),
         ]
-        where_x = jnp.broadcast_to(pair, (2 * CELL, chunk)).astype(BF16)
+        where_x = jnp.concatenate([pair, pair], axis=0).astype(BF16)
         one_hot = jnp.concatenate(
             [
                 jnp.where(
@@ -331,26 +354,26 @@
             tiles += [last_y * scaled, hat_y * (last_z * share)]
         corner = jnp.where(row_of == 0, shares[0], jnp.where(row_of == 1, shares[1], shares[2]))
         tiles.append(jnp.where(row_of < 3, corner * (last_y * last_z), 0.0))
-        pair_of = split(jnp.concatenate(tiles, axis=0))
-        return dot(jnp.concatenate(pair_of, axis=0), one_hot, ((1,), (1,)))
+        tiles.append(jnp.zeros(tall, F32))
+        return split(jnp.concatenate(tiles, axis=0)), one_hot
 
     turns = pos_ref.shape[1] // chunk
-    acc[...] = deposited(0)
-    if turns > 1:
-
-        @pl.loop(1, turns)
-        def _(turn_index):
-            acc[...] += deposited(turn_index)
+
+    acc[...] = jnp.zeros_like(acc)
+
+    @pl.loop(0, turns)
+    def _(index):
+        masses, one_hot = deposited(index)
+        for i in range(2):
+            acc[i] += dot(masses[i], one_hot, ((1,), (1,)))
 
     for load in loads[2:3]:
         load.wait()
-    sums = acc[...]
-    rows = sums.shape[0] // 2
-    sums = sums[:rows] + sums[rows:]
+    sums = acc[0] + acc[1]
     block = CELLS + 2 * CELL
     even = sums[:block] + pltpu.roll(sums[2 * block : 3 * block], 1, 1)
     odd = sums[block : 2 * block]
-    corner = sums[3 * block :]
+    corner = sums[3 * block : 3 * block + CELL]
     first = lax.broadcasted_iota(jnp.int32, (CELL, half), 0) == 0
     blank = jnp.zeros((CELL, half), F32)
     corner_even = corner + pltpu.roll(pltpu.roll(corner, CELL - 2, 0), 1, 1)
@@ -373,177 +396,207 @@
             for x in split(jnp.concatenate(folded, axis=1))
         ]
         both = dot_parts([line[parity, 0], line[parity, 1]], density, ((1,), (1,)))
-        for r in range(n // 2):
+        for r in range(n_own):
             re, im = both[r * nf : (r + 1) * nf], both[quarter + r * nf : quarter + (r + 1) * nf]
-            peer = parity * (n // 2) + r
-            send1[peer, 0:nf] = jnp.where(is_real, re[:, :128], im[:, :128])
+            send1[parity, r, 0:nf] = jnp.where(is_real, re[:, :128], im[:, :128])
             side = jnp.where(is_real_edge, re[:, 128:], im[:, 128:])
-            send1[peer, nf : nf + half_nf] = jnp.where(low_half, side[:half_nf], side[half_nf:])
-
-    pl.semaphore_wait(barrier, n - 1)
-
-    def start(source, target, send_sem, recv_sem):
-        @pl.loop(1, n)
-        def _(step):
-            peer, where = coords(step)
-            pltpu.make_async_remote_copy(
-                src_ref=source.at[peer],
-                dst_ref=target.at[rank],
-                send_sem=send_sem,
-                recv_sem=recv_sem,
+            send1[parity, r, nf : nf + half_nf] = jnp.where(
+                low_half, side[:half_nf], side[half_nf:]
+            )
+        if parity == 0:
+
+            @pl.when(is_owner)
+            def _():
+                pl.semaphore_wait(barrier, n - 1)
+
+            @pl.when(is_guest)
+            def _():
+                pl.semaphore_wait(barrier, n_own)
+
+        for maybe_self, peer, where in owners:
+            copy = pltpu.make_async_remote_copy(
+                src_ref=send1.at[parity, peer],
+                dst_ref=recv1.at[parity, rank],
+                send_sem=send_sem1.at[parity],
+                recv_sem=recv_sem1.at[parity],
                 device_id=where,
                 device_id_type=MESH,
-            ).start()
-
-        target[rank] = source[rank]
-
-    def finish_exchange(source, target, send_sem, recv_sem):
-        others = pl.ds(0, n - 1)
-        pltpu.make_async_copy(target.at[others], target.at[others], recv_sem).wait()
-        pltpu.make_async_copy(source.at[others], source.at[others], send_sem).wait()
-
-    with jax.named_scope("exch1"):
-        start(send1, recv1, send_sem1, recv_sem1)
-        green[...] = green_factor(rank, n_py, n_pz, nx, nf)
-        for load in loads[3:]:
-            load.wait()
-        with jax.named_scope("wait1"):
-            finish_exchange(send1, recv1, send_sem1, recv_sem1)
-
-    def at(ref, row):
-        return ref[row : row + 1]
+            )
+            if maybe_self:
+                pl.when(where[1] != my_z)(copy.start)
+            else:
+                copy.start()
+
+    def wait_for(ref, parity, count, sem):
+        span = ref.at[parity, pl.ds(0, count)]
+        pltpu.make_async_copy(span, span, sem.at[parity]).wait()
 
     def every(half_plane, py, pz):
         if pz <= n_pz // 2:
             return half_plane[py, pz], 1
         return half_plane[-py % n_py, n_pz - pz], -1
 
-    turned = []
-    for lanes, span, height in (
-        (slice(0, 128), slice(0, nf), nf),
-        (slice(128, 256), slice(nf, nf + half_nf), half_nf),
-    ):
-        values = [[recv1[ay * n_pz + az, span] for az in range(n_pz)] for ay in range(n_py)]
-        found = plane_forward(values, n_py, n_pz)
-        blocks = []
+    def middle(parity):
+        turned = []
+        for lanes, span, height in (
+            (slice(0, 128), slice(0, nf), nf),
+            (slice(128, 256), slice(nf, nf + half_nf), half_nf),
+        ):
+            values = [[recv1[parity, ay * n_pz + az, span] for az in range(n_pz)] for ay in range(n_py)]
+            found = plane_forward(values, n_py, n_pz)
+            blocks = []
+            for p in range(n):
+                (re, im), sign = every(found, p // n_pz, p % n_pz)
+                c, s = turn[p : p + 1, lanes], turn[n + p : n + p + 1, lanes]
+                if im is None:
+                    u, v = c * re, -(s * re)
+                elif sign > 0:
+                    u, v = c * re + s * im, c * im - s * re
+                else:
+                    u, v = c * re - s * im, -(c * im) - s * re
+                blocks.append([u, v])
+            turned.append(blocks)
+        if parity == 0:
+            corner_row = lax.broadcasted_iota(jnp.int32, (half_nf, 128), 0) == 0
+            top_row = lax.broadcasted_iota(jnp.int32, (nf, 128), 0) == 0
+            level = jnp.sum(turned[0][0][0][0:1] * jnp.where(is_real[0:1], 1.0, 0.0), axis=1, keepdims=True)
+            level += jnp.sum(
+                turned[1][0][0][0:1] * jnp.where(lane[0:1] < EDGE, 1.0, 0.0), axis=1, keepdims=True
+            )
+            level = jnp.where(owner == 0, level * (1.0 / CELLS), 0.0)
+            flat = turn[2 * n : 2 * n + 1]
+            turned[0][0][0] = turned[0][0][0] - jnp.where(top_row, level * flat[:, :128], 0.0)
+            turned[1][0][0] = turned[1][0][0] - jnp.where(corner_row, level * flat[:, 128:], 0.0)
+
+        stacked = [
+            jnp.concatenate(
+                [jnp.concatenate([uv[i] for uv in blocks], axis=0) for i in range(2)], axis=1
+            )
+            for blocks in turned
+        ]
+        high, low = split(stacked[0])
+        wide = dot(high, fwd[...])
+        solved = wide[:, :128] + wide[:, 128:] + dot(low, fwd[:, :128])
+        beside = dot_parts(split(stacked[1]), [fwd_edge[0], fwd_edge[1]])
+        pieces = []
         for p in range(n):
-            (re, im), sign = every(found, p // n_pz, p % n_pz)
-            c, s = turn[p : p + 1, lanes], turn[n + p : n + p + 1, lanes]
-            if im is None:
-                u, v = c * re, -(s * re)
-            elif sign > 0:
-                u, v = c * re + s * im, c * im - s * re
-            else:
-                u, v = c * re - s * im, -(c * im) - s * re
-            blocks.append([u, v])
-        turned.append(blocks)
-    corner_row = lax.broadcasted_iota(jnp.int32, (half_nf, 128), 0) == 0
-    top_row = lax.broadcasted_iota(jnp.int32, (nf, 128), 0) == 0
-    level = jnp.sum(turned[0][0][0][0:1] * jnp.where(is_real[0:1], 1.0, 0.0), axis=1, keepdims=True)
-    level += jnp.sum(
-        turned[1][0][0][0:1] * jnp.where(lane[0:1] < EDGE, 1.0, 0.0), axis=1, keepdims=True
-    )
-    level = jnp.where(rank == 0, level * (1.0 / CELLS), 0.0)
-    flat = turn[2 * n : 2 * n + 1]
-    turned[0][0][0] = turned[0][0][0] - jnp.where(top_row, level * flat[:, :128], 0.0)
-    turned[1][0][0] = turned[1][0][0] - jnp.where(corner_row, level * flat[:, 128:], 0.0)
-
-    stacked = [
-        jnp.concatenate(
-            [jnp.concatenate([uv[i] for uv in blocks], axis=0) for i in range(2)], axis=1
-        )
-        for blocks in turned
-    ]
-    high, low = split(stacked[0])
-    wide = dot(high, fwd[...])
-    solved = wide[:, :128] + wide[:, 128:] + dot(low, fwd[:, :128])
-    beside = dot_parts(split(stacked[1]), [fwd_edge[0], fwd_edge[1]])
-    pieces = []
-    for p in range(n):
-        rows_of = beside[p * half_nf : (p + 1) * half_nf]
-        pieces += [rows_of[:, :128], rows_of[:, 128:]]
-    solved = (solved + jnp.concatenate(pieces, axis=0)) * green[...]
-    high, low = split(solved)
-    mixed[...] = dot(jnp.concatenate([high, low], axis=1), inv[0:256]) + dot(high, inv[256:384])
-
-    for lanes, offset in ((slice(0, 128), 0), (slice(128, 256), 256)):
-        ones, twos = {}, {}
-        for p in range(n):
-            c, s = unturn[p : p + 1, lanes], unturn[n + p : n + p + 1, lanes]
-            span = slice(p * nf, (p + 1) * nf)
-            y, jy = mixed[span, offset : offset + 128], mixed[span, offset + 128 : offset + 256]
-            ones[p // n_pz, p % n_pz] = c * y + s * jy
-            twos[p // n_pz, p % n_pz] = c * jy - s * y
-        half_plane = {}
-        for pz in range(n_pz // 2 + 1):
-            for py in range(n_py):
-                other = (-py % n_py, -pz % n_pz)
-                if other == (py, pz):
-                    half_plane[py, pz] = (ones[other] * 2.0, None)
-                else:
-                    half_plane[py, pz] = (
-                        ones[py, pz] + ones[other],
-                        twos[other] - twos[py, pz],
-                    )
-        values = plane_inverse(half_plane, n_py, n_pz)
-        for ay in range(n_py):
-            for az in range(n_pz):
-                value = values[ay][az]
-                if offset == 0:
-                    send2[ay * n_pz + az] = value
-                else:
-                    value = jnp.where(low_half, value[:half_nf], value[half_nf:])
-                    send_edge[ay * n_pz + az] = value
-        if offset == 0:
-            start(send2, recv2, send_sem2, recv_sem2)
-        else:
-            start(send_edge, recv_edge, send_sem3, recv_sem3)
-
-    with jax.named_scope("wait2"):
-        finish_exchange(send2, recv2, send_sem2, recv_sem2)
-
-    def potential(columns):
-        found = [
-            dot_parts(split(columns[parity], 3), [back[parity, i] for i in range(3)])
-            for parity in range(2)
+            rows_of = beside[p * half_nf : (p + 1) * half_nf]
+            pieces += [rows_of[:, :128], rows_of[:, 128:]]
+        solved = (solved + jnp.concatenate(pieces, axis=0)) * green[parity]
+        high, low = split(solved)
+        mixed[...] = dot(jnp.concatenate([high, low], axis=1), inv[0:256]) + dot(high, inv[256:384])
+
+        for lanes, offset in ((slice(0, 128), 0), (slice(128, 256), 256)):
+            ones, twos = {}, {}
+            for p in range(n):
+                c, s = unturn[p : p + 1, lanes], unturn[n + p : n + p + 1, lanes]
+                span = slice(p * nf, (p + 1) * nf)
+                y, jy = mixed[span, offset : offset + 128], mixed[span, offset + 128 : offset + 256]
+                ones[p // n_pz, p % n_pz] = c * y + s * jy
+                twos[p // n_pz, p % n_pz] = c * jy - s * y
+            half_plane = {}
+            for pz in range(n_pz // 2 + 1):
+                for py in range(n_py):
+                    other = (-py % n_py, -pz % n_pz)
+                    if other == (py, pz):
+                        half_plane[py, pz] = (ones[other] * 2.0, None)
+                    else:
+                        half_plane[py, pz] = (
+                            ones[py, pz] + ones[other],
+                            twos[other] - twos[py, pz],
+                        )
+            values = plane_inverse(half_plane, n_py, n_pz)
+            for ay in range(n_py):
+                for az in range(n_pz):
+                    value = values[ay][az]
+                    if offset == 0:
+                        send2[parity, ay * n_pz + az, 0:nf] = value
+                    else:
+                        value = jnp.where(low_half, value[:half_nf], value[half_nf:])
+                        send2[parity, ay * n_pz + az, nf : nf + half_nf] = value
+        for peer, where in everyone:
+            pltpu.make_async_remote_copy(
+                src_ref=send2.at[parity, peer],
+                dst_ref=recv2.at[parity, owner],
+                send_sem=send_sem2.at[parity],
+                recv_sem=recv_sem2.at[parity],
+                device_id=where,
+                device_id_type=MESH,
+            ).start()
+        recv2[parity, owner] = send2[parity, rank]
+
+    @pl.when(is_owner)
+    def _():
+        for parity in range(2):
+            recv1[parity, rank] = send1[parity, owner]
+            green[parity] = green_factor(owner, parity, n_py, n_pz, nx, nf)
+        for load in loads[3:8]:
+            load.wait()
+        for parity in range(2):
+            with jax.named_scope("wait1"):
+                wait_for(recv1, parity, n - 1, recv_sem1)
+            with jax.named_scope("mid"):
+                middle(parity)
+
+    @pl.when(is_guest)
+    def _():
+        for load in loads[3:8]:
+            load.wait()
+
+    loads[8].wait()
+    found = []
+    for parity in range(2):
+        with jax.named_scope("wait2"):
+
+            @pl.when(is_owner)
+            def _():
+                wait_for(recv2, parity, n_own - 1, recv_sem2)
+
+            @pl.when(is_guest)
+            def _():
+                wait_for(recv2, parity, n_own, recv_sem2)
+
+        for r in range(n_own):
+            waves_edge[r * half_nf : (r + 1) * half_nf] = recv2[parity, r, nf : nf + half_nf]
+        beside = jnp.transpose(waves_edge[...])
+        rows_of = [
+            recv2[parity, r, h * half_nf : (h + 1) * half_nf]
+            for h in range(2)
+            for r in range(n_own)
         ]
-        return found[0] + found[1], found[0] - found[1]
-
-    columns = []
-    for parity in range(2):
-        peers = range(parity * (n // 2), (parity + 1) * (n // 2))
-        rows_of = [
-            recv2[r, h * half_nf : (h + 1) * half_nf] for h in range(2) for r in peers
-        ]
-        turned_back = jnp.transpose(jnp.concatenate(rows_of, axis=0))
-        columns.append(jnp.concatenate([turned_back[:CELLS], turned_back[CELLS:]], axis=1))
-    left, right = potential(columns)
-    for a in range(CELL):
-        pot_ref[a, :, :half] = left[a * CELL : (a + 1) * CELL]
-        pot_ref[a, :, half:] = right[a * CELL : (a + 1) * CELL]
-
-    with jax.named_scope("wait3"):
-        finish_exchange(send_edge, recv_edge, send_sem3, recv_sem3)
-    for r in range(n):
-        waves_edge[r * half_nf : (r + 1) * half_nf] = recv_edge[r]
-    turned_back = jnp.transpose(waves_edge[...])
-    columns = []
-    for parity in range(2):
-        span = slice(parity * CELLS, (parity + 1) * CELLS)
-        columns.append(
-            jnp.concatenate(
-                [
-                    turned_back[h * CELLS + c * EDGE : h * CELLS + (c + 1) * EDGE, span]
-                    for c in range(2)
-                    for h in range(2)
-                ],
-                axis=1,
+        inner = jnp.transpose(jnp.concatenate(rows_of, axis=0))
+        columns = []
+        for c in range(2):
+            pieces = [
+                beside[h * CELLS + c * EDGE : h * CELLS + (c + 1) * EDGE] for h in range(2)
+            ]
+            columns.append(
+                jnp.concatenate(
+                    [inner[c * CELLS : (c + 1) * CELLS], jnp.concatenate(pieces, axis=1)], axis=0
+                )
+            )
+        found.append(
+            dot_parts(
+                split(jnp.concatenate(columns, axis=1), 3), [back[parity, i] for i in range(3)]
             )
         )
-    left, right = potential(columns)
-    for i in range(4):
-        side_ref[i, :, :half] = left[i * CELL : (i + 1) * CELL]
-        side_ref[i, :, half:] = right[i * CELL : (i + 1) * CELL]
+    for side, value in enumerate((found[0] + found[1], found[0] - found[1])):
+        span = slice(side * half, (side + 1) * half)
+        for a in range(CELL):
+            pot_ref[a, :, span] = value[a * CELL : (a + 1) * CELL]
+        for i in range(4):
+            side_ref[i, :, span] = value[CELLS + i * CELL : CELLS + (i + 1) * CELL]
+
+    @pl.when(is_owner)
+    def _():
+        for parity in range(2):
+            wait_for(send1, parity, n_own - 1, send_sem1)
+            wait_for(send2, parity, n - 1, send_sem2)
+
+    @pl.when(is_guest)
+    def _():
+        for parity in range(2):
+            wait_for(send1, parity, n_own, send_sem1)
 
 
 def finish(pot_ref, side_ref, out_hbm, out_ref, sems):
@@ -579,7 +632,7 @@
     n_py, n_pz = mesh.shape["py"], mesh.shape["pz"]
     n = n_py * n_pz
     nx = 512
-    nf = nx // 2 // n
+    nf = nx // 4 // (n // 2)
     consts = tables(n_py, n_pz, nx, nf)
 
     def shards(positions, masses):
@@ -587,9 +640,8 @@
         vmem = pl.BlockSpec(memory_space=pltpu.VMEM)
         hbm = pl.BlockSpec(memory_space=pltpu.HBM)
         dma = pltpu.SemaphoreType.DMA
-        wide = pltpu.VMEM((n, nf + nf // 2, 128), F32)
-        block = pltpu.VMEM((n, nf, 128), F32)
-        edge = pltpu.VMEM((n, nf // 2, 128), F32)
+        rows = nf + nf // 2
+        few, all_of = (pltpu.VMEM((2, count, rows, 128), F32) for count in (n // 2, n))
         operands = [positions, masses.reshape(1, -1), *map(jnp.asarray, consts)]
         pot, side = pl.pallas_call(
             functools.partial(kernel, n_py, n_pz, nx, nf, chunk),
@@ -599,12 +651,12 @@
             scratch_shapes=[
                 *[pltpu.VMEM(x.shape, x.dtype) for x in operands],
                 dma((len(operands),)),
-                pltpu.VMEM((2 * (3 * (CELLS + 2 * CELL) + CELL), nx // 2), F32),
-                pltpu.VMEM((n * nf, 128), F32),
+                pltpu.VMEM((2, 3 * (CELLS + 2 * CELL) + 2 * CELL, nx // 2), F32),
+                pltpu.VMEM((2, n * nf, 128), F32),
                 pltpu.VMEM((n * nf, 512), F32),
-                wide, wide, block, block, edge, edge,
-                pltpu.VMEM((n * nf // 2, 128), F32),
-                dma, dma, dma, dma, dma, dma,
+                few, all_of, all_of, few,
+                pltpu.VMEM((n // 2 * (nf // 2), 128), F32),
+                dma((2,)), dma((2,)), dma((2,)), dma((2,)),
             ],
             compiler_params=pltpu.CompilerParams(
                 collective_id=0, has_side_effects=True, vmem_limit_bytes=50 << 20

time: 22.7 us -> 21.2 us (0.934)
  Pallas kernels: 22.5 us -> 21 us
    pallas_call x1, Pallas kernels: 21.6 us -> 20.1 us  [shards(): pl.pallas_call(functools.partial(kernel, n_py, n_pz, nx, nf, chunk), out_...]
where the time goes in v3:
time: 21.2 us; the launch traced here: 21 us
  Pallas kernels  21 us (99%)
    pallas_call x1, Pallas kernels, shards(): pl.pallas_call(functools.partial(kernel, n_py, n_pz, nx, nf, chunk), out_...  20.1 us
    pallas_call x1, Pallas kernels, shards(): pl.pallas_call(finish, out_shape=jax.ShapeDtypeStruct((3, CELL, CELL, nx)...  0.91 us

profile of v3, /device:TPU:0, one launch (start us, length us, event | category | flops | bytes accessed | tf_op | source)
XLA Modules:
  0.0 21.0 jit_solution(15308289760300811093)
XLA Ops:
  0.0 20.1 %shard_map.91 = (f32[8,8,512]{2,1,0:T(8,128)S(1)}, f32[4,8,512]{2,1,0:T(8,128)S(1)}) custom-call(f32[3,4096]{1,0:T(4,128)} %pos_hbm.1, f32[1,4096]{1,0:T(1,128)} %bitcast.1, bf16[2,2,256,256]{3,2,1,0:T(8,128)(2,1)} %constant.14.clone.line_hbm, bf16[2,3,256,256]{3,2,1,0:T(8,128)(2,1)} %constant.15.clone.back_hbm, bf16[256,256]{1,0:T(8,128)(2,1)} %constant.16.clone.fwd_hbm, ...), custom_call_target="tpu_custom_call" | custom-call | tf_op jit(solution)/shard_map/pallas_call | solution.py:646
  20.1 0.9 %shard_map.92 = f32[3,8,8,512]{3,2,1,0:T(8,128)} custom-call(f32[8,8,512]{2,1,0:T(8,128)S(1)} %get-tuple-element.7.pot_ref, f32[4,8,512]{2,1,0:T(8,128)S(1)} %get-tuple-element.8.side_ref), custom_call_target="tpu_custom_call" | custom-call | tf_op jit(solution)/shard_map/pallas_call | solution.py:665

commit v4 on v3

--- a/solution.py
+++ b/solution.py
@@ -281,10 +281,17 @@
         along = step % n_pz
         return -(along // 4), -bin(step).count("1"), along % 4 // 2, -step
 
-    everyone, owners = [], []
+    everyone, readers, owners = [], [], []
     for step in sorted(range(1, n), key=far_first):
         other_y, other_z = (step // n_pz) ^ my_y, (step % n_pz) ^ my_z
         everyone.append((other_y * n_pz + other_z, (other_y, other_z)))
+    core = lax.rem(my_z, 2)
+    for step in range(n):
+        along = step // (2 * n_py)
+        other_y, other_z = step // 2 % n_py, 2 * along + ((step % 2) ^ core)
+        if along:
+            other_y = other_y ^ my_y
+        readers.append((2 * along, other_y * n_pz + other_z, (other_y, other_z)))
     for step in sorted(range(n_own), key=lambda v: (-(v % half_z // 2), -bin(v // half_z).count("1"))):
         other_y, other_z = (step // half_z) ^ my_y, (step % half_z) ^ turn_z
         place = (other_y, other_z + first_z)
@@ -296,12 +303,6 @@
     def _():
         for _, where in everyone:
             pl.semaphore_signal(barrier, inc=1, device_id=where, device_id_type=MESH)
-
-    @pl.when(is_guest)
-    def _():
-        for _, _, where in owners:
-            pl.semaphore_signal(barrier, inc=1, device_id=where, device_id_type=MESH)
-
 
     for load in loads[2:]:
         load.start()
@@ -407,7 +408,7 @@
 
             @pl.when(is_owner)
             def _():
-                pl.semaphore_wait(barrier, n - 1)
+                pl.semaphore_wait(barrier, n_own - 1)
 
             @pl.when(is_guest)
             def _():
@@ -514,15 +515,19 @@
                     else:
                         value = jnp.where(low_half, value[:half_nf], value[half_nf:])
                         send2[parity, ay * n_pz + az, nf : nf + half_nf] = value
-        for peer, where in everyone:
-            pltpu.make_async_remote_copy(
+        for along, peer, where in readers:
+            copy = pltpu.make_async_remote_copy(
                 src_ref=send2.at[parity, peer],
                 dst_ref=recv2.at[parity, owner],
                 send_sem=send_sem2.at[parity],
                 recv_sem=recv_sem2.at[parity],
                 device_id=where,
                 device_id_type=MESH,
-            ).start()
+            )
+            if first_z <= along < first_z + half_z:
+                pl.when(peer != rank)(copy.start)
+            else:
+                copy.start()
         recv2[parity, owner] = send2[parity, rank]
 
     @pl.when(is_owner)

time: 21.2 us -> 20.1 us (0.948)
  Pallas kernels: 21 us -> 19.9 us
    pallas_call x1, Pallas kernels: 20.1 us -> 19 us  [shards(): pl.pallas_call(functools.partial(kernel, n_py, n_pz, nx, nf, chunk), out_...]
where the time goes in v4:
time: 20.1 us; the launch traced here: 19.9 us
  Pallas kernels  19.9 us (99%)
    pallas_call x1, Pallas kernels, shards(): pl.pallas_call(functools.partial(kernel, n_py, n_pz, nx, nf, chunk), out_...  19 us
    pallas_call x1, Pallas kernels, shards(): pl.pallas_call(finish, out_shape=jax.ShapeDtypeStruct((3, CELL, CELL, nx)...  0.91 us

profile of v4, /device:TPU:0, one launch (start us, length us, event | category | flops | bytes accessed | tf_op | source)
XLA Modules:
  0.0 19.9 jit_solution(1305830534151453603)
XLA Ops:
  0.0 19.0 %shard_map.91 = (f32[8,8,512]{2,1,0:T(8,128)S(1)}, f32[4,8,512]{2,1,0:T(8,128)S(1)}) custom-call(f32[3,4096]{1,0:T(4,128)} %pos_hbm.1, f32[1,4096]{1,0:T(1,128)} %bitcast.1, bf16[2,2,256,256]{3,2,1,0:T(8,128)(2,1)} %constant.14.clone.line_hbm, bf16[2,3,256,256]{3,2,1,0:T(8,128)(2,1)} %constant.15.clone.back_hbm, bf16[256,256]{1,0:T(8,128)(2,1)} %constant.16.clone.fwd_hbm, ...), custom_call_target="tpu_custom_call" | custom-call | tf_op jit(solution)/shard_map/pallas_call | solution.py:651
  19.0 0.9 %shard_map.92 = f32[3,8,8,512]{3,2,1,0:T(8,128)} custom-call(f32[8,8,512]{2,1,0:T(8,128)S(1)} %get-tuple-element.7.pot_ref, f32[4,8,512]{2,1,0:T(8,128)S(1)} %get-tuple-element.8.side_ref), custom_call_target="tpu_custom_call" | custom-call | tf_op jit(solution)/shard_map/pallas_call | solution.py:670

commit v5 on v4

--- a/solution.py
+++ b/solution.py
@@ -243,7 +243,7 @@
     pos_hbm, mass_hbm, line_hbm, back_hbm, fwd_hbm, fwd_edge_hbm, inv_hbm, turn_hbm, unturn_hbm,
     pot_ref, side_ref,
     pos_ref, mass_ref, line, back, fwd, fwd_edge, inv, turn, unturn, table_sem,
-    acc, green, mixed, send1, recv1, send2, recv2, waves_edge,
+    piece_sem, acc, green, mixed, send1, recv1, send2, recv2, waves_edge,
     send_sem1, recv_sem1, send_sem2, recv_sem2,
 ):
     n = n_py * n_pz
@@ -255,8 +255,6 @@
         pltpu.make_async_copy(src, dst, table_sem.at[i])
         for i, (src, dst) in enumerate(
             [
-                (pos_hbm, pos_ref),
-                (mass_hbm, mass_ref),
                 (line_hbm, line),
                 (turn_hbm, turn),
                 (fwd_hbm, fwd),
@@ -267,8 +265,15 @@
             ]
         )
     ]
-    for load in loads[:2]:
-        load.start()
+    pieces = []
+    width = pos_ref.shape[1] // 2
+    for i in range(2):
+        span = pl.ds(i * width, width)
+        for src, dst in ((pos_hbm, pos_ref), (mass_hbm, mass_ref)):
+            pieces.append(
+                pltpu.make_async_copy(src.at[:, span], dst.at[:, span], piece_sem.at[len(pieces)])
+            )
+            pieces[-1].start()
 
     n_own, half_z, first_z = n // 2, n_pz // 2, n_pz // 4
     own_z = my_z - first_z
@@ -288,9 +293,9 @@
     core = lax.rem(my_z, 2)
     for step in range(n):
         along = step // (2 * n_py)
-        other_y, other_z = step // 2 % n_py, 2 * along + ((step % 2) ^ core)
+        other_y, other_z = step // 2 % n_py, 2 * along + step % 2
         if along:
-            other_y = other_y ^ my_y
+            other_y, other_z = other_y ^ my_y, other_z ^ core
         readers.append((2 * along, other_y * n_pz + other_z, (other_y, other_z)))
     for step in sorted(range(n_own), key=lambda v: (-(v % half_z // 2), -bin(v // half_z).count("1"))):
         other_y, other_z = (step // half_z) ^ my_y, (step % half_z) ^ turn_z
@@ -304,7 +309,7 @@
         for _, where in everyone:
             pl.semaphore_signal(barrier, inc=1, device_id=where, device_id_type=MESH)
 
-    for load in loads[2:]:
+    for load in loads:
         load.start()
     base_y = (my_y * CELL).astype(F32)
     base_z = (my_z * CELL).astype(F32)
@@ -312,7 +317,7 @@
     cell = row_of.astype(F32)
     sublane = lax.broadcasted_iota(jnp.int32, (2 * CELL, chunk), 0).astype(F32)
 
-    for load in loads[:2]:
+    for load in pieces:
         load.wait()
 
     def deposited(turn_index):
@@ -368,7 +373,7 @@
         for i in range(2):
             acc[i] += dot(masses[i], one_hot, ((1,), (1,)))
 
-    for load in loads[2:3]:
+    for load in loads[:1]:
         load.wait()
     sums = acc[0] + acc[1]
     block = CELLS + 2 * CELL
@@ -515,19 +520,34 @@
                     else:
                         value = jnp.where(low_half, value[:half_nf], value[half_nf:])
                         send2[parity, ay * n_pz + az, nf : nf + half_nf] = value
-        for along, peer, where in readers:
-            copy = pltpu.make_async_remote_copy(
-                src_ref=send2.at[parity, peer],
-                dst_ref=recv2.at[parity, owner],
-                send_sem=send_sem2.at[parity],
-                recv_sem=recv_sem2.at[parity],
-                device_id=where,
-                device_id_type=MESH,
-            )
-            if first_z <= along < first_z + half_z:
-                pl.when(peer != rank)(copy.start)
-            else:
-                copy.start()
+        def deliver(which, chosen):
+            for along, peer, where in readers:
+                if along not in chosen:
+                    continue
+                copy = pltpu.make_async_remote_copy(
+                    src_ref=send2.at[which, peer],
+                    dst_ref=recv2.at[which, owner],
+                    send_sem=send_sem2.at[which],
+                    recv_sem=recv_sem2.at[which],
+                    device_id=where,
+                    device_id_type=MESH,
+                )
+                if first_z <= along < first_z + half_z:
+                    pl.when(peer != rank)(copy.start)
+                else:
+                    copy.start()
+
+        planes = list(range(0, n_pz, 2))
+        near, far = planes[:1], planes[-1:]
+        inner = planes[1:-1]
+        half_in = len(inner) // 2
+        if parity == 0:
+            deliver(0, near + far)
+        else:
+            deliver(1, near + far)
+            for along in inner:
+                deliver(0, [along])
+                deliver(1, [along])
         recv2[parity, owner] = send2[parity, rank]
 
     @pl.when(is_owner)
@@ -535,7 +555,7 @@
         for parity in range(2):
             recv1[parity, rank] = send1[parity, owner]
             green[parity] = green_factor(owner, parity, n_py, n_pz, nx, nf)
-        for load in loads[3:8]:
+        for load in loads[1:6]:
             load.wait()
         for parity in range(2):
             with jax.named_scope("wait1"):
@@ -545,10 +565,10 @@
 
     @pl.when(is_guest)
     def _():
-        for load in loads[3:8]:
+        for load in loads[1:6]:
             load.wait()
 
-    loads[8].wait()
+    loads[6].wait()
     found = []
     for parity in range(2):
         with jax.named_scope("wait2"):
@@ -656,6 +676,7 @@
             scratch_shapes=[
                 *[pltpu.VMEM(x.shape, x.dtype) for x in operands],
                 dma((len(operands),)),
+                dma((4,)),
                 pltpu.VMEM((2, 3 * (CELLS + 2 * CELL) + 2 * CELL, nx // 2), F32),
                 pltpu.VMEM((2, n * nf, 128), F32),
                 pltpu.VMEM((n * nf, 512), F32),

time: 20.1 us -> 19.4 us (0.965)
  Pallas kernels: 19.9 us -> 19.2 us
    pallas_call x1, Pallas kernels: 19 us -> 18.3 us  [shards(): pl.pallas_call(functools.partial(kernel, n_py, n_pz, nx, nf, chunk), out_...]
where the time goes in v5:
time: 19.4 us; the launch traced here: 19.2 us
  Pallas kernels  19.2 us (99%)
    pallas_call x1, Pallas kernels, shards(): pl.pallas_call(functools.partial(kernel, n_py, n_pz, nx, nf, chunk), out_...  18.3 us
    pallas_call x1, Pallas kernels, shards(): pl.pallas_call(finish, out_shape=jax.ShapeDtypeStruct((3, CELL, CELL, nx)...  0.91 us

profile of v5, /device:TPU:0, one launch (start us, length us, event | category | flops | bytes accessed | tf_op | source)
XLA Modules:
  0.0 19.2 jit_solution(6536885411604280008)
XLA Ops:
  0.0 18.3 %shard_map.91 = (f32[8,8,512]{2,1,0:T(8,128)S(1)}, f32[4,8,512]{2,1,0:T(8,128)S(1)}) custom-call(f32[3,4096]{1,0:T(4,128)} %pos_hbm.1, f32[1,4096]{1,0:T(1,128)} %bitcast.1, bf16[2,2,256,256]{3,2,1,0:T(8,128)(2,1)} %constant.14.clone.line_hbm, bf16[2,3,256,256]{3,2,1,0:T(8,128)(2,1)} %constant.15.clone.back_hbm, bf16[256,256]{1,0:T(8,128)(2,1)} %constant.16.clone.fwd_hbm, ...), custom_call_target="tpu_custom_call" | custom-call | tf_op jit(solution)/shard_map/pallas_call | solution.py:671
  18.3 0.9 %shard_map.92 = f32[3,8,8,512]{3,2,1,0:T(8,128)} custom-call(f32[8,8,512]{2,1,0:T(8,128)S(1)} %get-tuple-element.7.pot_ref, f32[4,8,512]{2,1,0:T(8,128)S(1)} %get-tuple-element.8.side_ref), custom_call_target="tpu_custom_call" | custom-call | tf_op jit(solution)/shard_map/pallas_call | solution.py:691

commit v6 on v5

--- a/solution.py
+++ b/solution.py
@@ -367,15 +367,16 @@
 
     acc[...] = jnp.zeros_like(acc)
 
-    @pl.loop(0, turns)
+    @pl.loop(0, turns // 2)
     def _(index):
-        masses, one_hot = deposited(index)
         for i in range(2):
-            acc[i] += dot(masses[i], one_hot, ((1,), (1,)))
+            masses, one_hot = deposited(2 * index + i)
+            acc[i] += dot(jnp.concatenate(masses, axis=0), one_hot, ((1,), (1,)))
 
     for load in loads[:1]:
         load.wait()
     sums = acc[0] + acc[1]
+    sums = sums[: sums.shape[0] // 2] + sums[sums.shape[0] // 2 :]
     block = CELLS + 2 * CELL
     even = sums[:block] + pltpu.roll(sums[2 * block : 3 * block], 1, 1)
     odd = sums[block : 2 * block]
@@ -480,9 +481,9 @@
             )
             for blocks in turned
         ]
-        high, low = split(stacked[0])
-        wide = dot(high, fwd[...])
-        solved = wide[:, :128] + wide[:, 128:] + dot(low, fwd[:, :128])
+        count = n * nf
+        wide = dot(jnp.concatenate(split(stacked[0]), axis=0), fwd[...])
+        solved = wide[:count, :128] + wide[:count, 128:] + wide[count:, :128]
         beside = dot_parts(split(stacked[1]), [fwd_edge[0], fwd_edge[1]])
         pieces = []
         for p in range(n):
@@ -661,7 +662,7 @@
     consts = tables(n_py, n_pz, nx, nf)
 
     def shards(positions, masses):
-        chunk = min(positions.shape[1], 2048)
+        chunk = positions.shape[1] // 2
         vmem = pl.BlockSpec(memory_space=pltpu.VMEM)
         hbm = pl.BlockSpec(memory_space=pltpu.HBM)
         dma = pltpu.SemaphoreType.DMA
@@ -677,7 +678,7 @@
                 *[pltpu.VMEM(x.shape, x.dtype) for x in operands],
                 dma((len(operands),)),
                 dma((4,)),
-                pltpu.VMEM((2, 3 * (CELLS + 2 * CELL) + 2 * CELL, nx // 2), F32),
+                pltpu.VMEM((2, 2 * (3 * (CELLS + 2 * CELL) + 2 * CELL), nx // 2), F32),
                 pltpu.VMEM((2, n * nf, 128), F32),
                 pltpu.VMEM((n * nf, 512), F32),
                 few, all_of, all_of, few,

time: 19.4 us -> 19.3 us (level)
  no operation moved by 1% of the time
where the time goes in v6:
time: 19.3 us; the launch traced here: 19.1 us
  Pallas kernels  19.1 us (99%)
    pallas_call x1, Pallas kernels, shards(): pl.pallas_call(functools.partial(kernel, n_py, n_pz, nx, nf, chunk), out_...  18.2 us
    pallas_call x1, Pallas kernels, shards(): pl.pallas_call(finish, out_shape=jax.ShapeDtypeStruct((3, CELL, CELL, nx)...  0.91 us

profile of v6, /device:TPU:0, one launch (start us, length us, event | category | flops | bytes accessed | tf_op | source)
XLA Modules:
  0.0 19.1 jit_solution(1556491157737430764)
XLA Ops:
  0.0 18.2 %shard_map.91 = (f32[8,8,512]{2,1,0:T(8,128)S(1)}, f32[4,8,512]{2,1,0:T(8,128)S(1)}) custom-call(f32[3,4096]{1,0:T(4,128)} %pos_hbm.1, f32[1,4096]{1,0:T(1,128)} %bitcast.1, bf16[2,2,256,256]{3,2,1,0:T(8,128)(2,1)} %constant.14.clone.line_hbm, bf16[2,3,256,256]{3,2,1,0:T(8,128)(2,1)} %constant.15.clone.back_hbm, bf16[256,256]{1,0:T(8,128)(2,1)} %constant.16.clone.fwd_hbm, ...), custom_call_target="tpu_custom_call" | custom-call | tf_op jit(solution)/shard_map/pallas_call | solution.py:672
  18.2 0.9 %shard_map.92 = f32[3,8,8,512]{3,2,1,0:T(8,128)} custom-call(f32[8,8,512]{2,1,0:T(8,128)S(1)} %get-tuple-element.7.pot_ref, f32[4,8,512]{2,1,0:T(8,128)S(1)} %get-tuple-element.8.side_ref), custom_call_target="tpu_custom_call" | custom-call | tf_op jit(solution)/shard_map/pallas_call | solution.py:692
